TPU v7x, 16 devices: a 4x2x1 block of a 4x4x8 slice. The times are simulated.
16 devices in a mesh: batch: 2 (over y, z), dap: 8 (over x, core).
Axes of the slice: x: 4, y: 2, z: 1, core: 2. Of those that a mesh axis runs over, the one named last changes fastest.
The devices are a block of a 4x4x8 slice.
Arguments:
- z_pair: bfloat16 [1024, 512, 64], P(('batch', 'dap')), parts along dimension 0
- pair_mask: int32 [1024, 512], P(('batch', 'dap')), parts along dimension 0
- dz_out: bfloat16 [1024, 512, 64], P(('batch', 'dap')), parts along dimension 0
- ln_in_scale: bfloat16 [64], replicated
- ln_in_offset: bfloat16 [64], replicated
- w_in: bfloat16 [64, 256], replicated
- b_in: bfloat16 [256], replicated
- ln_out_scale: bfloat16 [64], replicated
- ln_out_offset: bfloat16 [64], replicated
- w_out: bfloat16 [64, 64], replicated
- b_out: bfloat16 [64], replicated
- w_gate: bfloat16 [64, 64], replicated
- b_gate: bfloat16 [64], replicated
Outputs:
- output 1: bfloat16 [1024, 512, 64], P(('batch', 'dap')), parts along dimension 0
- output 2: bfloat16 [128], P('batch'), parts along dimension 0
- output 3: bfloat16 [128], P('batch'), parts along dimension 0
- output 4: bfloat16 [128, 256], P('batch'), parts along dimension 0
- output 5: bfloat16 [512], P('batch'), parts along dimension 0
- output 6: bfloat16 [128], P('batch'), parts along dimension 0
- output 7: bfloat16 [128], P('batch'), parts along dimension 0
- output 8: bfloat16 [128, 64], P('batch'), parts along dimension 0
- output 9: bfloat16 [128], P('batch'), parts along dimension 0
- output 10: bfloat16 [128, 64], P('batch'), parts along dimension 0
- output 11: bfloat16 [128], P('batch'), parts along dimension 0
There are 2 independent parts. A program takes and returns all parts, laid end to end along the dimension named above; an argument that names none is the same for every part.
All inputs are finite; a program needn't handle non-finite values.
Results may differ from a plain program's by a relative error of at most 0.0152256.
Values are sent between devices in bfloat16 or wider.
A program may use at most 768 MiB of HBM per device.

v0:
```python
import jax
import jax.numpy as jnp
from jax import lax
from jax.sharding import PartitionSpec as P

LN_EPS = 1e-5


def norm_forward(x_val, ln_scale, ln_offset, axis_id):
    mean_val = jnp.mean(x_val, axis=axis_id, keepdims=True)
    centered = x_val - mean_val
    inv_std = lax.rsqrt(jnp.mean(centered * centered, axis=axis_id, keepdims=True) + LN_EPS)
    x_hat = centered * inv_std
    return x_hat, inv_std, x_hat * ln_scale + ln_offset


def norm_backward(grad_out, x_hat, inv_std, ln_scale, axis_id):
    grad_hat = grad_out * ln_scale
    mean_grad = jnp.mean(grad_hat, axis=axis_id, keepdims=True)
    mean_proj = jnp.mean(grad_hat * x_hat, axis=axis_id, keepdims=True)
    return inv_std * (grad_hat - mean_grad - x_hat * mean_proj)


def input_side(z_part, mask_part, ln_in_scale, ln_in_offset, w_in, b_in):
    hidden = w_in.shape[1] // 4
    in_hat, in_inv, in_aff = norm_forward(z_part.astype(jnp.float32), ln_in_scale.astype(jnp.float32), ln_in_offset.astype(jnp.float32), -1)
    z_norm = in_aff.astype(jnp.bfloat16)
    proj_t = jnp.einsum('de,rnd->ern', w_in, z_norm, preferred_element_type=jnp.float32) + b_in.astype(jnp.float32)[:, None, None]
    proj_a = proj_t[:hidden]
    proj_b = proj_t[hidden:2 * hidden]
    sig_a = jax.nn.sigmoid(proj_t[2 * hidden:3 * hidden])
    sig_b = jax.nn.sigmoid(proj_t[3 * hidden:])
    mask_f = mask_part.astype(jnp.float32)[None]
    act_a = (mask_f * sig_a * proj_a).astype(jnp.bfloat16)
    act_b = (mask_f * sig_b * proj_b).astype(jnp.bfloat16)
    return in_hat, in_inv, z_norm, proj_a, proj_b, sig_a, sig_b, mask_f, act_a, act_b


def output_chain(tri_out, gate_lin, dy_part, ln_out_scale, ln_out_offset, w_out, b_out):
    out_scale = ln_out_scale.astype(jnp.float32)[:, None, None]
    out_offset = ln_out_offset.astype(jnp.float32)[:, None, None]
    out_hat, out_inv, out_aff = norm_forward(tri_out, out_scale, out_offset, 0)
    o_norm = out_aff.astype(jnp.bfloat16)
    update = (jnp.einsum('crn,cd->rnd', o_norm, w_out, preferred_element_type=jnp.float32) + b_out.astype(jnp.float32)).astype(jnp.bfloat16)
    sig_g = jax.nn.sigmoid(gate_lin)
    dy_f = dy_part.astype(jnp.float32)
    d_update = (sig_g * dy_f).astype(jnp.bfloat16)
    d_gate_lin = dy_f * update.astype(jnp.float32) * sig_g * (1.0 - sig_g)
    d_onorm = jnp.einsum('cd,rnd->crn', w_out, d_update, preferred_element_type=jnp.float32).astype(jnp.bfloat16).astype(jnp.float32)
    d_tri = norm_backward(d_onorm, out_hat, out_inv, out_scale, 0).astype(jnp.bfloat16)
    return d_tri, o_norm, out_hat, d_onorm, d_update, d_gate_lin


def input_backward(d_act_a, d_act_b, proj_a, proj_b, sig_a, sig_b, mask_f, z_norm, in_hat, in_inv, dy_part, d_gate_lin, ln_in_scale, w_in, w_gate):
    grad_a = d_act_a.astype(jnp.bfloat16).astype(jnp.float32) * mask_f
    grad_b = d_act_b.astype(jnp.bfloat16).astype(jnp.float32) * mask_f
    d_proj = jnp.concatenate([grad_a * sig_a, grad_b * sig_b, grad_a * proj_a * sig_a * (1.0 - sig_a), grad_b * proj_b * sig_b * (1.0 - sig_b)], axis=0)
    d_b_in = jnp.sum(d_proj, axis=(1, 2))
    d_b_gate = jnp.sum(d_gate_lin, axis=(0, 1))
    proj_grad16 = d_proj.astype(jnp.bfloat16)
    gate_grad16 = d_gate_lin.astype(jnp.bfloat16)
    d_w_in = jnp.einsum('rnd,ern->de', z_norm, proj_grad16, preferred_element_type=jnp.float32)
    d_w_gate = jnp.einsum('rnd,rne->de', z_norm, gate_grad16, preferred_element_type=jnp.float32)
    d_znorm = (jnp.einsum('ern,de->rnd', proj_grad16, w_in, preferred_element_type=jnp.float32) + jnp.einsum('rne,de->rnd', gate_grad16, w_gate, preferred_element_type=jnp.float32)).astype(jnp.bfloat16).astype(jnp.float32)
    d_in_scale = jnp.sum(d_znorm * in_hat, axis=(0, 1))
    d_in_offset = jnp.sum(d_znorm, axis=(0, 1))
    d_z = (dy_part.astype(jnp.float32) + norm_backward(d_znorm, in_hat, in_inv, ln_in_scale.astype(jnp.float32), -1)).astype(jnp.bfloat16)
    return d_z, d_in_scale, d_in_offset, d_w_in, d_b_in, d_w_gate, d_b_gate


def local_grads(z_loc, mask_loc, dy_loc, ln_in_scale, ln_in_offset, w_in, b_in, ln_out_scale, ln_out_offset, w_out, b_out, w_gate, b_gate):
    in_hat, in_inv, z_norm, proj_a, proj_b, sig_a, sig_b, mask_f, act_a, act_b = input_side(z_loc, mask_loc, ln_in_scale, ln_in_offset, w_in, b_in)
    gate_lin = jnp.einsum('rnd,de->rne', z_norm, w_gate, preferred_element_type=jnp.float32) + b_gate.astype(jnp.float32)
    b_full = lax.all_gather(act_b, 'dap', axis=1, tiled=True)
    tri_out = jnp.einsum('cik,cjk->cij', act_a, b_full, preferred_element_type=jnp.float32)
    d_tri, o_norm, out_hat, d_onorm, d_update, d_gate_lin = output_chain(tri_out, gate_lin, dy_loc, ln_out_scale, ln_out_offset, w_out, b_out)
    d_w_out = jnp.einsum('crn,rnd->cd', o_norm, d_update, preferred_element_type=jnp.float32)
    d_b_out = jnp.sum(d_update.astype(jnp.float32), axis=(0, 1))
    d_out_scale = jnp.sum(d_onorm * out_hat, axis=(1, 2))
    d_out_offset = jnp.sum(d_onorm, axis=(1, 2))
    d_act_a = jnp.einsum('cij,cjk->cik', d_tri, b_full, preferred_element_type=jnp.float32)
    d_b_part = jnp.einsum('cij,cik->cjk', d_tri, act_a, preferred_element_type=jnp.float32)
    d_act_b = lax.psum_scatter(d_b_part, 'dap', scatter_dimension=1, tiled=True)
    d_z, d_in_scale, d_in_offset, d_w_in, d_b_in, d_w_gate, d_b_gate = input_backward(d_act_a, d_act_b, proj_a, proj_b, sig_a, sig_b, mask_f, z_norm, in_hat, in_inv, dy_loc, d_gate_lin, ln_in_scale, w_in, w_gate)
    summed = lax.psum((d_in_scale, d_in_offset, d_w_in, d_b_in, d_out_scale, d_out_offset, d_w_out, d_b_out, d_w_gate, d_b_gate), 'dap')
    return (d_z,) + tuple(grad_piece.astype(jnp.bfloat16) for grad_piece in summed)


def solution(mesh):
    pair_spec = P(('batch', 'dap'), None, None)
    mask_spec = P(('batch', 'dap'), None)
    vec_rep = P(None)
    mat_rep = P(None, None)
    vec_part = P('batch')
    mat_part = P('batch', None)
    in_specs = (pair_spec, mask_spec, pair_spec, vec_rep, vec_rep, mat_rep, vec_rep, vec_rep, vec_rep, mat_rep, vec_rep, mat_rep, vec_rep)
    out_specs = (pair_spec, vec_part, vec_part, mat_part, vec_part, vec_part, vec_part, mat_part, vec_part, mat_part, vec_part)
    return jax.shard_map(local_grads, mesh=mesh, in_specs=in_specs, out_specs=out_specs, check_vma=False)
```

profile of v0, /device:TPU:112, one launch (start us, length us, event | category | flops | bytes accessed | tf_op | source)
XLA Modules:
  0.0 795.3 jit_solution(16049135720092249765)
XLA Ops:
  7.2 0.0 copy-start
  7.2 0.1 all-gather.2.cloned.1.call-start
  7.3 0.0 copy-start.2
  7.3 0.8 convert_element_type.129
  8.1 0.8 convert_element_type.130
  8.9 0.7 convert_element_type.132
  9.6 0.9 convert_element_type.128
  10.5 3.4 convert_reduce_fusion.2
  13.9 3.9 fusion.22
  17.8 13.5 %add_bitcast_fusion = f32[256,64,512]{2,0,1:T(8,128)} fusion(f32[256]{0:T(256)S(1)} %convert_element_type.132, bf16[64,256]{1,0:T(8,128)(2,1)S(1)} %copy-done, bf16[64,512,64]{1,2,0:T(8,128)(2,1)S(1)} %copy-done.2, f32[64]{0:T(128)S(1)} %convert_element_type.130, f32[64]{0:T(128)S(1)} %convert_element_type.129, f32[64,512]{1,0:T(8,128)S(1)} %add_rsqrt_fusion.1, ...), kind=kOutput, calls=%fused_computation.1 | convolution fusion | flops 1094713344 | bytes 38045184 | tf_op jit(solution)/shard_map/de,rnd->ern/dot_general | solution.py:28
  31.3 0.0 copy-start.12
  31.3 17.0 %multiply_convert_fusion.1 = (bf16[64,64,512]{2,0,1:T(8,128)(2,1)}, bf16[64,64,512]{2,0,1:T(8,128)(2,1)}) fusion(f32[256,64,512]{2,0,1:T(8,128)} %add_bitcast_fusion, f32[64,512]{1,0:T(8,128)S(1)} %convert_element_type.128), kind=kLoop, calls=%fused_computation.69 | loop fusion | flops 25165824 | bytes 42074112 | tf_op jit(solution)/shard_map/convert_element_type | solution.py:34
  48.4 0.1 all-gather.2.cloned.1.call-update
  48.4 0.5 reduce-scatter.2.cloned.1.call-start
  49.0 0.0 copy-start.11
  49.1 9.6 %convert_reduce_fusion.3 = (f32[64]{0:T(128)}, bf16[64,512,64]{1,2,0:T(8,128)(2,1)S(1)}, f32[64,512,64]{1,2,0:T(8,128)}) fusion(bf16[64,512,64]{1,2,0:T(8,128)(2,1)} %param.15, f32[64]{0:T(128)S(1)} %convert_element_type.135, bf16[64,64]{1,0:T(8,128)(2,1)S(1)} %copy-done.12, bf16[64,512,64]{1,2,0:T(8,128)(2,1)} %param.13, f32[64]{0:T(128)S(1)} %convert_element_type.130, ...), kind=kOutput, calls=%fused_computation.56 | convolution fusion | flops 299892672 | bytes 21242880 | tf_op jit(solution)/shard_map/rnd,de->rne/dot_general | solution.py:73
  58.6 2.0 copy-done.7
  60.6 1.2 fusion.64
  61.8 10.6 %convert_reduce_fusion.1 = (f32[64]{0:T(128)}, bf16[64,512,64]{1,0,2:T(8,128)(2,1)}) fusion(bf16[64,512,64]{1,2,0:T(8,128)(2,1)S(1)} %fusion.64), kind=kLoop, calls=%fused_computation.17 | loop fusion | flops 4194240 | bytes 8388864 | tf_op jit(solution)/shard_map/reduce_sum | solution.py:80
  72.5 131.7 %all-gather.2.cloned.1.call-done = bf16[64,512,512]{2,0,1:T(8,128)(2,1)} async-done(((bf16[64,64,512]{2,0,1:T(8,128)(2,1)}), bf16[64,512,512]{2,0,1:T(8,128)(2,1)}) %all-gather.2.cloned.1.call-update) | async-done | bytes 33554448 | tf_op jit(solution)/shard_map/all_gather | solution.py:74
  204.1 45.7 %fusion.71 = (f32[64,512]{1,0:T(8,128)S(1)}, f32[64,64,512]{2,1,0:T(8,128)}) fusion(bf16[64,512,512]{2,0,1:T(8,128)(2,1)} %all-gather.2.cloned.1.call-done, bf16[64,64,512]{2,0,1:T(8,128)(2,1)} %get-tuple-element.38), kind=kOutput, calls=%fused_computation.100 | convolution fusion | flops 2149548032 | bytes 46268416 | tf_op jit(solution)/shard_map/cik,cjk->cij/dot_general | solution.py:75
  249.9 4.7 multiply_reduce_fusion
  254.6 1.0 copy-done.1
  255.6 5.0 fusion.27
  260.7 5.9 fusion.25
  266.6 33.5 %fusion.46 = f32[64,512,512]{2,1,0:T(8,128)} fusion(bf16[64,64,512]{2,1,0:T(8,128)(2,1)} %get-tuple-element.40, bf16[64,64,512]{2,0,1:T(8,128)(2,1)} %get-tuple-element.38), kind=kOutput, calls=%fused_computation.75 | convolution fusion | flops 2147483648 | bytes 75497472 | tf_op jit(solution)/shard_map/cij,cik->cjk/dot_general | solution.py:82
  300.1 56.6 %copy.42 = f32[64,512,512]{2,0,1:T(8,128)} copy(f32[64,512,512]{2,1,0:T(8,128)} %fusion.46) | data formatting | bytes 134217728 | tf_op jit(solution)/shard_map/cij,cik->cjk/dot_general | solution.py:82
  356.7 0.0 copy-start.19
  356.7 0.1 reduce-scatter.2.cloned.1.call-update
  356.7 0.6 copy-done.19
  357.3 10.7 %fusion.72 = (f32[64]{0:T(128)S(1)}, bf16[64,512,64]{1,2,0:T(8,128)(2,1)S(1)}) fusion(f32[64,512,64]{1,2,0:T(8,128)} %get-tuple-element.42, f32[64]{0:T(128)S(1)} %convert_element_type.149, bf16[64,64]{1,0:T(8,128)(2,1)S(1)} %copy-done.11, bf16[64,64,512]{2,1,0:T(8,128)(2,1)} %get-tuple-element.41, bf16[64,512,64]{1,2,0:T(8,128)(2,1)} %param.15), kind=kOutput, calls=%fused_computation.101 | convolution fusion | flops 289406912 | bytes 20980224 | tf_op jit(solution)/shard_map/crn,cd->rnd/dot_general | solution.py:44
  368.1 0.0 copy-start.3
  368.1 5.5 fusion.53
  373.6 0.9 copy-done.8
  374.5 5.0 fusion.58
  379.5 0.0 copy-start.5
  379.5 2.0 fusion.55
  381.5 0.2 copy-done.5
  381.7 32.9 %fusion = bf16[64,64,512]{2,1,0:T(8,128)(2,1)} fusion(bf16[64,64,512]{2,1,0:T(8,128)(2,1)S(1)} %copy-done.5, bf16[64,512,512]{2,0,1:T(8,128)(2,1)} %all-gather.2.cloned.1.call-done), kind=kOutput, calls=%fused_computation.2 | convolution fusion | flops 2147483648 | bytes 41943040 | tf_op jit(solution)/shard_map/cij,cjk->cik/dot_general | solution.py:81
  414.6 266.9 %reduce-scatter.2.cloned.1.call-done = f32[64,64,512]{2,0,1:T(8,128)} async-done(((f32[64,512,512]{2,0,1:T(8,128)}), f32[64,64,512]{2,0,1:T(8,128)}) %reduce-scatter.2.cloned.1.call-update) | async-done | bytes 8388624 | tf_op jit(solution)/shard_map/reduce_scatter | solution.py:83
  681.5 27.1 %fusion.41 = (f32[64,64,512]{2,0,1:T(8,128)}, f32[64,64,512]{2,0,1:T(8,128)}, f32[64,64,512]{2,0,1:T(8,128)}, f32[64,64,512]{2,0,1:T(8,128)}) fusion(f32[64,512]{1,0:T(8,128)S(1)} %copy-done.10, bf16[64,64,512]{2,1,0:T(8,128)(2,1)} %fusion, f32[256,64,512]{2,0,1:T(8,128)} %add_bitcast_fusion, f32[64,64,512]{2,0,1:T(8,128)} %reduce-scatter.2.cloned.1.call-done), kind=kLoop, calls=%fused_computation.65 | loop fusion | flops 44040192 | bytes 79822848 | tf_op jit(solution)/shard_map/mul | solution.py:57
  708.7 11.6 %fusion.4 = f32[256]{0:T(256)S(1)} fusion(f32[64,64,512]{2,0,1:T(8,128)} %get-tuple-element.36, f32[64,64,512]{2,0,1:T(8,128)} %get-tuple-element.35, f32[64,64,512]{2,0,1:T(8,128)} %get-tuple-element.37, f32[64,64,512]{2,0,1:T(8,128)} %get-tuple-element.34), kind=kLoop, calls=%fused_computation.6 | loop fusion | flops 33554176 | bytes 33555456 | tf_op jit(solution)/shard_map/reduce_sum | solution.py:58
  720.3 13.8 %convolution_bitcast_fusion = f32[64,256]{1,0:T(8,128)S(1)} fusion(f32[64,64,512]{2,0,1:T(8,128)} %get-tuple-element.36, f32[64,64,512]{2,0,1:T(8,128)} %get-tuple-element.35, f32[64,64,512]{2,0,1:T(8,128)} %get-tuple-element.37, f32[64,64,512]{2,0,1:T(8,128)} %get-tuple-element.34, bf16[64,512,64]{1,2,0:T(8,128)(2,1)} %param.13, ...), kind=kOutput, calls=%fused_computation.82 | convolution fusion | flops 1153433600 | bytes 38076928 | tf_op jit(solution)/shard_map/rnd,ern->de/dot_general | solution.py:62
  734.1 18.8 %fusion.33 = (f32[64]{0:T(128)S(1)}, f32[64,512]{1,0:T(8,128)S(1)}, f32[64,512]{1,0:T(8,128)S(1)}, f32[64]{0:T(128)S(1)}, bf16[64,512,64]{1,2,0:T(8,128)(2,1)}) fusion(bf16[64,512,64]{1,2,0:T(8,128)(2,1)} %param.13, f32[64,512]{1,0:T(8,128)S(1)} %add_rsqrt_fusion.1, f32[64,512]{1,0:T(8,128)S(1)} %broadcast_multiply_fusion.5, ...), kind=kOutput, calls=%fused_computation.45 | convolution fusion | flops 1168048128 | bytes 50889472 | tf_op jit(solution)/shard_map/ern,de->rnd/dot_general | solution.py:64
  753.0 0.0 copy-start.14
  753.0 0.0 copy-start.15
  753.1 8.5 %fusion.32 = bf16[64,512,64]{1,2,0:T(8,128)(2,1)} fusion(bf16[64,512,64]{1,2,0:T(8,128)(2,1)} %param.13, bf16[64,512,64]{1,2,0:T(8,128)(2,1)} %get-tuple-element.45, bf16[64,512,64]{1,2,0:T(8,128)(2,1)} %param.15, f32[64,512]{1,0:T(8,128)S(1)} %broadcast_multiply_fusion, f32[64,512]{1,0:T(8,128)S(1)} %broadcast_multiply_fusion.1, ...), kind=kLoop, calls=%fused_computation.44 | loop fusion | flops 25165824 | bytes 17301760 | tf_op jit(solution)/shard_map/convert_element_type | solution.py:67
  761.5 26.5 %all-reduce = (bf16[64]{0:T(256)(128)(2,1)}, bf16[64]{0:T(256)(128)(2,1)}, bf16[64,256]{1,0:T(8,128)(2,1)}, bf16[256]{0:T(256)(128)(2,1)}, bf16[64]{0:T(256)(128...) all-reduce(f32[64]{0:T(128)S(1)} %get-tuple-element.13, ...), channel_id=1, replica_groups=mesh['batch'=2,'dap'=8] {'dap'}, use_global_device_ids=true, to_apply=%region_10.0 | all-reduce | flops 25216 | bytes 151296 | tf_op jit(solution)/shard_map/psum | solution.py:85
  (37 shorter events, 0.2 us)
Async XLA Ops:
  7.2 10.6 %copy-start = (bf16[64,256]{1,0:T(8,128)(2,1)S(1)}, bf16[64,256]{1,0:T(8,128)(2,1)}, u32[]{:S(2)}) copy-start(bf16[64,256]{1,0:T(8,128)(2,1)} %param.18) | copy-start | bytes 98308
  7.2 196.9 %all-gather.2.cloned.1.call-start = ((), (), s32[]{:S(2)}) async-start(), calls=%async_computation.1 | async-start | bytes 37748736 | tf_op jit(solution)/shard_map/all_gather | solution.py:74
  7.3 10.6 %copy-start.2 = (bf16[64,512,64]{1,2,0:T(8,128)(2,1)S(1)}, bf16[64,512,64]{1,2,0:T(8,128)(2,1)}, u32[]{:S(2)}) copy-start(bf16[64,512,64]{1,2,0:T(8,128)(2,1)} %param.13) | copy-start | bytes 12582916
  10.5 20.8 %copy-start.9 = (f32[64,512]{1,0:T(8,128)}, f32[64,512]{1,0:T(8,128)S(1)}, u32[]{:S(2)}) copy-start(f32[64,512]{1,0:T(8,128)S(1)} %convert_element_type.128) | copy-start | bytes 393220
  31.3 17.7 %copy-start.16 = (bf16[64]{0:T(256)(128)(2,1)S(1)}, bf16[64]{0:T(256)(128)(2,1)}, u32[]{:S(2)}) copy-start(bf16[64]{0:T(256)(128)(2,1)} %param.20) | copy-start | bytes 388
  31.3 17.7 %copy-start.17 = (bf16[64]{0:T(256)(128)(2,1)S(1)}, bf16[64]{0:T(256)(128)(2,1)}, u32[]{:S(2)}) copy-start(bf16[64]{0:T(256)(128)(2,1)} %param.21) | copy-start | bytes 388
  31.3 17.7 %copy-start.18 = (bf16[64]{0:T(256)(128)(2,1)S(1)}, bf16[64]{0:T(256)(128)(2,1)}, u32[]{:S(2)}) copy-start(bf16[64]{0:T(256)(128)(2,1)} %param.25) | copy-start | bytes 388
  31.3 17.7 %copy-start.12 = (bf16[64,64]{1,0:T(8,128)(2,1)S(1)}, bf16[64,64]{1,0:T(8,128)(2,1)}, u32[]{:S(2)}) copy-start(bf16[64,64]{1,0:T(8,128)(2,1)} %param.24) | copy-start | bytes 24580
  48.4 633.1 %reduce-scatter.2.cloned.1.call-start = ((), (), s32[]{:S(2)}) async-start(), calls=%async_computation.2 | async-start | bytes 75497472 | tf_op jit(solution)/shard_map/reduce_scatter | solution.py:83
  49.0 11.6 %copy-start.11 = (bf16[64,64]{1,0:T(8,128)(2,1)S(1)}, bf16[64,64]{1,0:T(8,128)(2,1)}, u32[]{:S(2)}) copy-start(bf16[64,64]{1,0:T(8,128)(2,1)} %param.22) | copy-start | bytes 24580
  58.6 2.0 copy-start.7
  204.1 50.5 %copy-start.4 = (bf16[64,512,64]{1,0,2:T(8,128)(2,1)S(1)}, bf16[64,512,64]{1,0,2:T(8,128)(2,1)}, u32[]{:S(2)}) copy-start(bf16[64,512,64]{1,0,2:T(8,128)(2,1)} %get-tuple-element.31) | copy-start | bytes 12582916
  249.9 5.8 copy-start.1
  356.7 0.7 copy-start.19
  368.1 5.5 copy-start.6
  368.1 6.4 copy-start.8
  368.1 11.4 %copy-start.3 = (bf16[64,512,64]{1,2,0:T(8,128)(2,1)S(1)}, bf16[64,512,64]{1,2,0:T(8,128)(2,1)}, u32[]{:S(2)}) copy-start(bf16[64,512,64]{1,2,0:T(8,128)(2,1)} %param.13) | copy-start | bytes 12582916
  379.5 2.2 copy-start.5
  381.7 299.9 %copy-start.10 = (f32[64,512]{1,0:T(8,128)S(1)}, f32[64,512]{1,0:T(8,128)}, u32[]{:S(2)}) copy-start(f32[64,512]{1,0:T(8,128)} %copy-done.9) | copy-start | bytes 393220
  753.0 8.5 %copy-start.13 = (f32[64]{0:T(128)S(1)}, f32[64]{0:T(128)}, u32[]{:S(2)}) copy-start(f32[64]{0:T(128)} %get-tuple-element.30) | copy-start | bytes 772
  753.0 8.5 %copy-start.14 = (f32[64]{0:T(128)S(1)}, f32[64]{0:T(128)}, u32[]{:S(2)}) copy-start(f32[64]{0:T(128)} %get-tuple-element.11) | copy-start | bytes 772
  753.0 8.5 %copy-start.15 = (f32[64]{0:T(128)S(1)}, f32[64]{0:T(128)}, u32[]{:S(2)}) copy-start(f32[64]{0:T(128)} %get-tuple-element.28) | copy-start | bytes 772
Sparse Core Ops, SparseCore 0:
  48.6 155.5 all-gather.1
  356.9 324.6 reduce-scatter.1
where the time goes:
time: 802 us; the launch traced here: 795 us
  waiting for transfers between devices  399 us (50%)
  matrix products  192 us (24%)
  other arithmetic  101 us (13%)
  local copies, waits for them, and re-layouts  61.3 us (8%)
  blocking collectives  26.5 us (3%)
  between operations  14.8 us (2%)
    reduce_scatter x1, waiting for transfers between devices, local_grads(): d_act_b = lax.psum_scatter(d_b_part, 'dap', scatter_dimension=1, tiled=True)  267 us
    all_gather x1, waiting for transfers between devices, local_grads(): b_full = lax.all_gather(act_b, 'dap', axis=1, tiled=True)  132 us
    dot_general x1, local copies, waits for them, and re-layouts, local_grads(): jnp.einsum('cij,cik->cjk', d_tri, act_a, preferred_element_type=jnp.float32)  56.6 us
    dot_general x1, matrix products, local_grads(): jnp.einsum('cik,cjk->cij', act_a, b_full, preferred_element_type=jnp.floa...  45.7 us
    dot_general x1, matrix products, local_grads(): jnp.einsum('cij,cik->cjk', d_tri, act_a, preferred_element_type=jnp.float32)  33.5 us
    dot_general x1, matrix products, local_grads(): jnp.einsum('cij,cjk->cik', d_tri, b_full, preferred_element_type=jnp.floa...  32.9 us
    mul x1, other arithmetic, input_backward(): grad_a * sig_a  27.1 us
    psum x1, blocking collectives, local_grads(): lax.psum((d_in_scale, d_in_offset, d_w_in, d_b_in, d_out_scale, d_out_off...  26.5 us
  transfers between devices with their start and end apart: 2, of which 2 were waited for; matrix products, arithmetic and copies ran while one was open for 10% of the time, Pallas kernels for 0%

commit v1 on v0

v1 whole, which is shorter than its diff:
```python
import functools
import jax
import jax.numpy as jnp
from jax import lax
from jax.experimental import pallas as pl
from jax.experimental.pallas import tpu as pltpu
from jax.sharding import PartitionSpec as P

LN_EPS = 1e-5
F32 = jnp.float32
BF16 = jnp.bfloat16
SUB = 8
VMEM_LIMIT = 63 * 1024 * 1024


def nn_dot(lhs, rhs):
    return lax.dot_general(lhs, rhs, (((1,), (0,)), ((), ())), preferred_element_type=F32)


def nt_dot(lhs, rhs):
    return lax.dot_general(lhs, rhs, (((1,), (1,)), ((), ())), preferred_element_type=F32)


def tn_dot(lhs, rhs):
    return lax.dot_general(lhs, rhs, (((0,), (0,)), ((), ())), preferred_element_type=F32)


def row_norm(z8, scale, offset):
    mean_val = jnp.mean(z8, axis=1, keepdims=True)
    centered = z8 - mean_val
    inv_std = lax.rsqrt(jnp.mean(centered * centered, axis=1, keepdims=True) + LN_EPS)
    z_hat = centered * inv_std
    return z_hat, inv_std, (z_hat * scale[None] + offset[None]).astype(BF16)


def lanes(bias, width):
    return jnp.concatenate([bias] * (width // bias.shape[-1]), axis=-1)


def gated(prod, bias_ref, start, chans, mask_half):
    cols = prod.shape[-1]
    val = prod[:chans * SUB].reshape(chans, SUB, cols) + lanes(bias_ref[start:start + chans], cols)
    gate = prod[chans * SUB:].reshape(chans, SUB, cols) + lanes(bias_ref[start + chans:start + 2 * chans], cols)
    return (jnp.tanh(gate) + 1.0) * (val * mask_half[None])


def own_kernel(z_ref, dy_ref, mask_ref, wk_ref, bias_ref, gk_ref, gbias_ref, perm_ref, sc_ref, off_ref, a_ref, lg_ref, dyt_ref):
    chans = a_ref.shape[0]
    cols = z_ref.shape[-1]
    a_parts, dy_parts = [], []
    for half in range(2):
        rows = slice(half * SUB, (half + 1) * SUB)
        _, _, zn = row_norm(z_ref[rows].astype(F32), sc_ref[...], off_ref[...])
        zn2 = zn.reshape(SUB * zn.shape[1], cols)
        mask_half = mask_ref[rows].astype(F32) * 0.5
        a_parts.append(gated(nn_dot(wk_ref[...], zn2), bias_ref, 0, chans, mask_half))
        lg = nn_dot(gk_ref[...], zn2).reshape(chans, SUB, cols) + lanes(gbias_ref[...], cols)
        lg_ref[:, rows, :] = lg
        dy2 = dy_ref[rows].reshape(SUB * dy_ref.shape[1], cols)
        dy_parts.append(nn_dot(perm_ref[...], dy2).reshape(chans, SUB, cols))
    a_ref[...] = jnp.concatenate(a_parts, axis=1).astype(BF16)
    dyt_ref[...] = jnp.concatenate(dy_parts, axis=1).astype(BF16)


def all_kernel(*refs):
    z_ref, mask_ref, wka_ref, wkb_ref, ba_ref, bb_ref, sc_ref, off_ref = refs[:8]
    a_ref, b_ref = refs[-2:]
    cols = z_ref.shape[-1]
    a_parts, b_parts = [], []
    for half in range(2):
        rows = slice(half * SUB, (half + 1) * SUB)
        _, _, zn = row_norm(z_ref[0, rows].astype(F32), sc_ref[...], off_ref[...])
        zn2 = zn.reshape(SUB * zn.shape[1], cols)
        mask_half = mask_ref[0, rows].astype(F32) * 0.5
        a_parts.append(gated(nn_dot(wka_ref[...], zn2), ba_ref, 0, a_ref.shape[0], mask_half))
        b_parts.append(gated(nn_dot(wkb_ref[...], zn2), bb_ref, 0, b_ref.shape[0], mask_half))
    a_ref[...] = jnp.concatenate(a_parts, axis=1).astype(BF16)
    b_ref[...] = jnp.concatenate(b_parts, axis=1).astype(BF16)


def chain_kernel(a_ref, b_ref, lg_ref, dyt_ref, wo_ref, wot_ref, bout_ref, sc_ref, off_ref,
                 do_ref, dgl_ref, da_ref, gram_ref, dbg_ref, dbo_ref, dsc_ref, dof_ref, o_s, da_s):
    chans, rows, _ = a_ref.shape
    jb = b_ref.shape[1]
    step = pl.program_id(0)

    @pl.when(step == 0)
    def _():
        da_s[...] = jnp.zeros_like(da_s)
        for ref in (gram_ref, dbg_ref, dbo_ref, dsc_ref, dof_ref):
            ref[...] = jnp.zeros_like(ref)

    def o_body(c, carry):
        o_s[c] = nt_dot(a_ref[c], b_ref[c])
        return carry
    lax.fori_loop(0, chans, o_body, 0, unroll=4)

    def chain_body(g, carry):
        dgl_parts, dt_parts = [], []
        for half in range(2):
            r0 = pl.multiple_of(g * 2 * SUB + half * SUB, SUB)
            o8 = o_s[:, pl.ds(r0, SUB), :]
            centered = o8 - jnp.mean(o8, axis=0, keepdims=True)
            inv_std = lax.rsqrt(jnp.mean(centered * centered, axis=0, keepdims=True) + LN_EPS)
            o_hat = centered * inv_std
            o_norm = (o_hat * sc_ref[...] + off_ref[...]).astype(BF16).reshape(chans * SUB, jb)
            upd = (nn_dot(wo_ref[...], o_norm).reshape(chans, SUB, jb) + bout_ref[...]).astype(BF16).astype(F32)
            sig = jnp.tanh(lg_ref[:, pl.ds(r0, SUB), :] * 0.5) * 0.5 + 0.5
            dyf = dyt_ref[:, pl.ds(pl.multiple_of(g * 2 * SUB, 2 * SUB), 2 * SUB), :].astype(F32)[:, half * SUB:(half + 1) * SUB]
            prod = sig * dyf
            d_upd = prod.astype(BF16)
            dgl = prod * upd * (1.0 - sig)
            dbg_ref[...] += dgl
            dgl_parts.append(dgl)
            dbo_ref[...] += d_upd.astype(F32)
            d_upd2 = d_upd.reshape(chans * SUB, jb)
            gram_ref[...] += nt_dot(o_norm, d_upd2)
            d_on = nn_dot(wot_ref[...], d_upd2).astype(BF16).astype(F32).reshape(chans, SUB, jb)
            dsc_ref[...] += d_on * o_hat
            dof_ref[...] += d_on
            g_hat = d_on * sc_ref[...]
            m1 = jnp.mean(g_hat, axis=0, keepdims=True)
            m2 = jnp.mean(g_hat * o_hat, axis=0, keepdims=True)
            dt_parts.append(inv_std * (g_hat - m1 - o_hat * m2))
        pair = pl.ds(pl.multiple_of(g * 2 * SUB, 2 * SUB), 2 * SUB)
        dgl_ref[:, pair, :] = jnp.concatenate(dgl_parts, axis=1).astype(BF16)
        do_ref[0, :, pair, :] = jnp.concatenate(dt_parts, axis=1).astype(BF16)
        return carry
    lax.fori_loop(0, rows // (2 * SUB), chain_body, 0)

    def da_body(c, carry):
        da_s[c] += nn_dot(do_ref[0, c], b_ref[c])
        return carry
    lax.fori_loop(0, chans, da_body, 0, unroll=4)

    @pl.when(step == pl.num_programs(0) - 1)
    def _():
        da_ref[...] = da_s[...].astype(BF16)


def db_kernel(do_ref, a_ref, db_ref):
    per = do_ref.shape[1]
    for c in range(per):
        lhs = do_ref[:, c].reshape(do_ref.shape[0] * do_ref.shape[2], do_ref.shape[3])
        db_ref[c] = tn_dot(lhs, a_ref[c]).astype(BF16)


def input_kernel(z_ref, dy_ref, mask_ref, da_ref, db_ref, dgl_ref, wk_ref, bias_ref, wg_ref, sc_ref, off_ref,
                 dz_ref, gram_ref, dbias_ref, dsc_ref, dof_ref, dp_s):
    chans = da_ref.shape[0]
    chan_z, cols = z_ref.shape[1:]

    @pl.when(pl.program_id(0) == 0)
    def _():
        for ref in (gram_ref, dbias_ref, dsc_ref, dof_ref):
            ref[...] = jnp.zeros_like(ref)

    def fold(val):
        acc = val[..., :128]
        for lane in range(128, cols, 128):
            acc = acc + val[..., lane:lane + 128]
        return acc

    n_p = chans * SUB
    for half in range(2):
        rows = slice(half * SUB, (half + 1) * SUB)
        z_hat, inv_std, zn = row_norm(z_ref[rows].astype(F32), sc_ref[...], off_ref[...])
        zn2 = zn.reshape(SUB * chan_z, cols)
        mask_f = mask_ref[rows].astype(F32)[None]
        for side, grad_ref in enumerate((da_ref, db_ref)):
            prod = nn_dot(wk_ref[side * 2 * n_p:(side + 1) * 2 * n_p], zn2)
            val = prod[:n_p].reshape(chans, SUB, cols) + lanes(bias_ref[side * 2 * chans:side * 2 * chans + chans], cols)
            gate = prod[n_p:].reshape(chans, SUB, cols) + lanes(bias_ref[side * 2 * chans + chans:(side + 1) * 2 * chans], cols)
            sig = jnp.tanh(gate) * 0.5 + 0.5
            grad = grad_ref[...].astype(F32)[:, rows] * mask_f
            d_val = grad * sig
            d_gate = d_val * val * (1.0 - sig)
            dbias_ref[side * chans:(side + 1) * chans] += fold(d_val)
            dbias_ref[(side + 2) * chans:(side + 3) * chans] += fold(d_gate)
            dp_s[side * n_p:(side + 1) * n_p] = d_val.astype(BF16).reshape(n_p, cols)
            dp_s[(side + 2) * n_p:(side + 3) * n_p] = d_gate.astype(BF16).reshape(n_p, cols)
        dp_s[4 * n_p:] = dgl_ref[...].astype(F32)[:, rows].astype(BF16).reshape(n_p, cols)
        d_zn = nn_dot(wg_ref[...], dp_s[...]).astype(BF16).astype(F32).reshape(SUB, chan_z, cols)
        gram = nt_dot(zn2, dp_s[...]).reshape(SUB, chan_z, dp_s.shape[0])
        lane_row = lax.broadcasted_iota(jnp.int32, (chan_z, dp_s.shape[0]), 1) % SUB
        acc = gram_ref[...]
        for i in range(SUB):
            acc = acc + jnp.where(lane_row == i, gram[i], 0.0)
        gram_ref[...] = acc
        dsc_ref[...] += jnp.sum(d_zn * z_hat, axis=0)
        dof_ref[...] += jnp.sum(d_zn, axis=0)
        g_hat = d_zn * sc_ref[...][None]
        m1 = jnp.mean(g_hat, axis=1, keepdims=True)
        m2 = jnp.mean(g_hat * z_hat, axis=1, keepdims=True)
        d_z = dy_ref[rows].astype(F32) + inv_std * (g_hat - m1 - z_hat * m2)
        dz_ref[rows] = d_z.astype(BF16)


def spread(w_t):
    eye = jnp.eye(SUB, dtype=w_t.dtype)
    return (w_t[:, None, None, :] * eye[None, :, :, None]).reshape(w_t.shape[0] * SUB, SUB * w_t.shape[1])


def same_rows(w_t):
    eye = jnp.eye(SUB, dtype=w_t.dtype)
    return (w_t[:, None, :, None] * eye[None, :, None, :]).reshape(w_t.shape[0] * SUB, SUB * w_t.shape[1])


def vec8(vec):
    return jnp.broadcast_to(vec.astype(F32)[:, None, None], (vec.shape[0], SUB, 128))


def whole(arr):
    nd = arr.ndim
    return pl.BlockSpec(arr.shape, lambda *_: (0,) * nd, pipeline_mode=pl.Buffered(1))


def params(**kw):
    return pltpu.CompilerParams(vmem_limit_bytes=VMEM_LIMIT, **kw)


def local_grads(n_dap, z_loc, mask_loc, dy_loc, ln_in_scale, ln_in_offset, w_in, b_in, ln_out_scale, ln_out_offset, w_out, b_out, w_gate, b_gate):
    rows, cols, cz = z_loc.shape
    ch = w_in.shape[1] // 4
    half = ch // 2
    total = rows * n_dap
    jb = 2 * rows
    sds = jax.ShapeDtypeStruct
    core = lax.axis_index('dap') % 2
    z_t = jnp.transpose(z_loc, (0, 2, 1))
    dy_t = jnp.transpose(dy_loc, (0, 2, 1))

    w_t = w_in.T
    w_pa, w_pb, w_la, w_lb = w_t[:ch], w_t[ch:2 * ch], w_t[2 * ch:3 * ch] * 0.5, w_t[3 * ch:] * 0.5
    b_pa, b_pb, b_la, b_lb = b_in[:ch], b_in[ch:2 * ch], b_in[2 * ch:3 * ch] * 0.5, b_in[3 * ch:] * 0.5
    mine = lambda arr: lax.dynamic_slice_in_dim(arr, core * half, half, 0)
    wk_a = spread(jnp.concatenate([w_pa, w_la]))
    wk_b = spread(jnp.concatenate([w_pb, w_lb]))
    wk_ah = spread(jnp.concatenate([mine(w_pa), mine(w_la)]))
    bias_a = vec8(jnp.concatenate([b_pa, b_la]))
    bias_b = vec8(jnp.concatenate([b_pb, b_lb]))
    bias_ah = vec8(jnp.concatenate([mine(b_pa), mine(b_la)]))
    sc_in = jnp.broadcast_to(ln_in_scale.astype(F32)[:, None], (cz, cols))
    off_in = jnp.broadcast_to(ln_in_offset.astype(F32)[:, None], (cz, cols))
    gk = spread(w_gate.T)
    perm = spread(jnp.eye(cz, dtype=BF16))

    grp = 2 * SUB
    n_grp = rows // grp
    chunks = []
    for q in range(n_grp):
        piece = z_t[q * grp:(q + 1) * grp]
        if q == 0:
            piece = jnp.concatenate([piece, mask_loc.astype(BF16).reshape(rows // cz, cz, cols)], axis=0)
        chunks.append(lax.all_gather(piece, 'dap', axis=0))
    mask_all = chunks[0][:, grp:].reshape(n_dap, rows, cols)

    row3 = lambda nd: pl.BlockSpec((grp, nd, cols), lambda g: (g, 0, 0))
    chan_rows = lambda n: pl.BlockSpec((n, grp, cols), lambda g: (0, g, 0))
    mask_spec = pl.BlockSpec((grp, cols), lambda g: (g, 0))
    args = (z_t, dy_t, mask_loc, wk_a, bias_a, gk, vec8(b_gate), perm, sc_in, off_in)
    a_own, lg, dyt = pl.pallas_call(
        own_kernel, grid=(n_grp,), name='own_rows',
        out_shape=(sds((ch, rows, cols), BF16), sds((cz, rows, cols), F32), sds((cz, rows, cols), BF16)),
        in_specs=[row3(cz), row3(cz), mask_spec] + [whole(x) for x in args[3:]],
        out_specs=(chan_rows(ch), chan_rows(cz), chan_rows(cz)),
        cost_estimate=pl.CostEstimate(flops=10**10, bytes_accessed=30 * 2**20, transcendentals=0),
        compiler_params=params())(*args)

    a_half = b_full = None
    for q in range(n_grp):
        args = (chunks[q], mask_all, wk_ah, wk_b, bias_ah, bias_b, sc_in, off_in)
        specs = [pl.BlockSpec((1, grp, cz, cols), lambda p: (p, 0, 0, 0)),
                 pl.BlockSpec((1, grp, cols), lambda p, q=q: (p, q, 0))] + [whole(x) for x in args[2:]]
        alias = {}
        if q:
            args = args + (a_half, b_full)
            specs = specs + [pl.BlockSpec(memory_space=pl.ANY)] * 2
            alias = {8: 0, 9: 1}
        a_half, b_full = pl.pallas_call(
            all_kernel, grid=(n_dap,), name=f'all_rows_{q}',
            out_shape=(sds((half, total, cols), BF16), sds((ch, total, cols), BF16)),
            in_specs=specs,
            out_specs=(pl.BlockSpec((half, grp, cols), lambda p, q=q: (0, p * n_grp + q, 0)),
                       pl.BlockSpec((ch, grp, cols), lambda p, q=q: (0, p * n_grp + q, 0))),
            input_output_aliases=alias,
            cost_estimate=pl.CostEstimate(flops=2 * 10**10, bytes_accessed=30 * 2**20, transcendentals=0),
            compiler_params=params())(*args)

    sc_out, off_out = vec8(ln_out_scale), vec8(ln_out_offset)
    args = (a_own, b_full, lg, dyt, same_rows(w_out.T), same_rows(w_out), vec8(b_out), sc_out, off_out)
    acc_shape = sds((ch, SUB, 128), F32)
    acc_spec = pl.BlockSpec((ch, SUB, 128), lambda j: (0, 0, 0))
    col_spec = pl.BlockSpec((ch, rows, jb), lambda j: (0, 0, j))
    gram_n = ch * SUB
    do_blk, dgl, da, gram_o, dbg, dbo, dsc_o, dof_o = pl.pallas_call(
        chain_kernel, grid=(total // jb,), name='chain',
        out_shape=(sds((total // jb, ch, rows, jb), BF16), sds((cz, rows, cols), BF16), sds((ch, rows, cols), BF16),
                   sds((gram_n, gram_n), F32), acc_shape, acc_shape, acc_shape, acc_shape),
        in_specs=[whole(a_own), pl.BlockSpec((ch, jb, cols), lambda j: (0, j, 0)), col_spec, col_spec] + [whole(x) for x in args[4:]],
        out_specs=(pl.BlockSpec((1, ch, rows, jb), lambda j: (j, 0, 0, 0)), col_spec,
                   pl.BlockSpec((ch, rows, cols), lambda j: (0, 0, 0), pipeline_mode=pl.Buffered(1)),
                   pl.BlockSpec((gram_n, gram_n), lambda j: (0, 0)), acc_spec, acc_spec, acc_spec, acc_spec),
        scratch_shapes=[pltpu.VMEM((ch, rows, jb), F32), pltpu.VMEM((ch, rows, cols), F32)],
        cost_estimate=pl.CostEstimate(flops=2 * 10**10, bytes_accessed=60 * 2**20, transcendentals=0),
        compiler_params=params())(*args)

    do_all = lax.all_to_all(do_blk.reshape(n_dap, half, rows, jb), 'dap', 0, 0)
    per = 4
    db_pair = pl.pallas_call(
        db_kernel, grid=(half // per,), name='db',
        out_shape=sds((half, jb, cols), BF16),
        in_specs=[pl.BlockSpec((n_dap, per, rows, jb), lambda c: (0, c, 0, 0)),
                  pl.BlockSpec((per, total, cols), lambda c: (c, 0, 0))],
        out_specs=pl.BlockSpec((per, jb, cols), lambda c: (c, 0, 0)),
        cost_estimate=pl.CostEstimate(flops=10**10, bytes_accessed=30 * 2**20, transcendentals=0),
        compiler_params=params())(do_all, a_half)
    keep = lax.dynamic_slice_in_dim(db_pair, core * rows, rows, 1)
    give = lax.dynamic_slice_in_dim(db_pair, (1 - core) * rows, rows, 1)
    got = lax.ppermute(give, 'dap', [(i, i ^ 1) for i in range(n_dap)])
    low = core == 0
    db = jnp.concatenate([jnp.where(low, keep, got), jnp.where(low, got, keep)], axis=0)

    w_back = jnp.concatenate([w_in, w_gate], axis=1)
    eye = jnp.eye(SUB, dtype=BF16)
    wg = (w_back[None, :, :, None] * eye[:, None, None, :]).reshape(SUB * cz, w_back.shape[1] * SUB)
    args = (z_t, dy_t, mask_loc, da, db, dgl, jnp.concatenate([wk_a, wk_b]), jnp.concatenate([bias_a, bias_b]), wg, sc_in, off_in)
    n_e = w_back.shape[1]
    const = lambda *shape: pl.BlockSpec(shape, lambda g: (0,) * len(shape))
    dz_t, gram_i, dbias, dsc_i, dof_i = pl.pallas_call(
        input_kernel, grid=(n_grp,), name='input_side',
        out_shape=(sds((rows, cz, cols), BF16), sds((cz, n_e * SUB), F32), sds((4 * ch, SUB, 128), F32),
                   sds((cz, cols), F32), sds((cz, cols), F32)),
        in_specs=[row3(cz), row3(cz), mask_spec, chan_rows(ch), chan_rows(ch), chan_rows(cz)] + [whole(x) for x in args[6:]],
        out_specs=(row3(cz), const(cz, n_e * SUB), const(4 * ch, SUB, 128), const(cz, cols), const(cz, cols)),
        scratch_shapes=[pltpu.VMEM((n_e * SUB, cols), BF16)],
        cost_estimate=pl.CostEstimate(flops=10**10, bytes_accessed=30 * 2**20, transcendentals=0),
        compiler_params=params())(*args)

    d_w = gram_i.reshape(cz, n_e, SUB).sum(-1)
    d_wout = jnp.einsum('cidi->cd', gram_o.reshape(ch, SUB, cz, SUB))
    tail = lambda acc: acc.sum((-2, -1))
    partial = (dsc_i.sum(-1), dof_i.sum(-1), d_w[:, :4 * ch], tail(dbias), tail(dsc_o), tail(dof_o), d_wout, tail(dbo), d_w[:, 4 * ch:], tail(dbg))
    summed = lax.psum(partial, 'dap')
    return (jnp.transpose(dz_t, (0, 2, 1)),) + tuple(piece.astype(BF16) for piece in summed)


def solution(mesh):
    pair_spec = P(('batch', 'dap'), None, None)
    mask_spec = P(('batch', 'dap'), None)
    vec_rep = P(None)
    mat_rep = P(None, None)
    vec_part = P('batch')
    mat_part = P('batch', None)
    in_specs = (pair_spec, mask_spec, pair_spec, vec_rep, vec_rep, mat_rep, vec_rep, vec_rep, vec_rep, mat_rep, vec_rep, mat_rep, vec_rep)
    out_specs = (pair_spec, vec_part, vec_part, mat_part, vec_part, vec_part, vec_part, mat_part, vec_part, mat_part, vec_part)
    body = functools.partial(local_grads, mesh.shape['dap'])
    return jax.shard_map(body, mesh=mesh, in_specs=in_specs, out_specs=out_specs, check_vma=False)
```

time: 802 us -> 494 us (0.62)
  waiting for transfers between devices: 399 us -> 101 us
  Pallas kernels: 0 us -> 225 us
  matrix products: 192 us -> 0 us
  other arithmetic: 101 us -> 36.1 us
  local copies, waits for them, and re-layouts: 61.3 us -> 80.5 us
    reduce_scatter x1 -> x0, waiting for transfers between devices: 267 us -> none  [local_grads(): d_act_b = lax.psum_scatter(d_b_part, 'dap', scatter_dimension=1, tiled=True)]
    pallas_call x0 -> x8, Pallas kernels: none -> 225 us  [the longest x4 89.8 us: local_grads(): pl.pallas_call(all_kernel, grid=(n_dap,), name=f'all_rows_{q}', out_shape...]
    dot_general x12 -> x0, matrix products: 192 us -> none  [the longest x1 45.7 us: local_grads(): jnp.einsum('cik,cjk->cij', act_a, b_full, preferred_element_type=jnp.floa...]
    all_gather x1 -> x4, waiting for transfers between devices: 132 us -> 49.9 us  [local_grads(): chunks.append(lax.all_gather(piece, 'dap', axis=0))]
    dot_general x1 -> x0, local copies, waits for them, and re-layouts: 56.6 us -> none  [local_grads(): jnp.einsum('cij,cik->cjk', d_tri, act_a, preferred_element_type=jnp.float32)]
    all_to_all x0 -> x1, waiting for transfers between devices: none -> 49.4 us  [local_grads(): do_all = lax.all_to_all(do_blk.reshape(n_dap, half, rows, jb), 'dap', 0, 0)]
    mul x0 -> x9, local copies, waits for them, and re-layouts: none -> 48.6 us  [the longest x2 27.1 us: same_rows(): w_t[:, None, :, None] * eye[None, :, None, :]]
    convert_element_type x11 -> x5, other arithmetic: 34.7 us -> 0.24 us  [the longest x3 0.22 us: vec8(): vec.astype(F32)[:, None, None]]
  transfers between devices with their start and end apart: 2 -> 6, of which waited for: 2 -> 4; matrix products, arithmetic and copies ran while one was open for 10% -> 19% of each run, Pallas kernels for 0% -> 17%
where the time goes in v1:
time: 494 us; the launch traced here: 490 us
  Pallas kernels  225 us (46%)
  waiting for transfers between devices  101 us (20%)
  local copies, waits for them, and re-layouts  80.5 us (16%)
  other arithmetic  36.1 us (7%)
  blocking collectives  27.8 us (6%)
  between operations  14.3 us (3%)
  starting transfers between devices  5.19 us (1%)
    pallas_call x4, Pallas kernels, local_grads(): pl.pallas_call(all_kernel, grid=(n_dap,), name=f'all_rows_{q}', out_shape...  89.8 us
    pallas_call x1, Pallas kernels, local_grads(): pl.pallas_call(chain_kernel, grid=(total // jb,), name='chain', out_shape...  65.7 us
    all_gather x4, waiting for transfers between devices, local_grads(): chunks.append(lax.all_gather(piece, 'dap', axis=0))  49.9 us
    all_to_all x1, waiting for transfers between devices, local_grads(): do_all = lax.all_to_all(do_blk.reshape(n_dap, half, rows, jb), 'dap', 0, 0)  49.4 us
    pallas_call x1, Pallas kernels, local_grads(): pl.pallas_call(input_kernel, grid=(n_grp,), name='input_side', out_shape=...  41.7 us
    psum x1, blocking collectives, local_grads(): summed = lax.psum(partial, 'dap')  27.8 us
    mul x2, local copies, waits for them, and re-layouts, same_rows(): w_t[:, None, :, None] * eye[None, :, None, :]  27.1 us
    pallas_call x1, Pallas kernels, local_grads(): pl.pallas_call(own_kernel, grid=(n_grp,), name='own_rows', out_shape=(sds...  16 us
  transfers between devices with their start and end apart: 6, of which 4 were waited for; matrix products, arithmetic and copies ran while one was open for 19% of the time, Pallas kernels for 17%

profile of v1, /device:TPU:112, one launch (start us, length us, event | category | flops | bytes accessed | tf_op | source)
XLA Modules:
  0.0 490.4 jit_solution(3647935815704286017)
XLA Ops:
  7.3 4.0 fusion.2
  11.3 1.2 pad_maximum_fusion.2
  12.6 0.7 all-gather.15.cloned.1.call-update
  15.4 1.2 broadcast_multiply_fusion.5
  16.6 1.4 mul.176.refs_2_
  18.6 1.7 broadcast_multiply_fusion.3
  20.3 4.6 mul.180.refs_3_
  24.8 2.5 mul.169.gk_ref
  27.4 1.4 mul.172.perm_ref
  28.8 2.0 mul.164.wk_ref
  30.9 6.4 %broadcast_multiply_fusion = (bf16[64,8,64,8]{3,2,1,0:T(8,128)(2,1)}, bf16[64,8,64,8]{3,2,1,0:T(8,128)(2,1)}) fusion(bf16[64,64]{1,0:T(8,128)(2,1)S(1)} %copy-done.12, bf16[8,8]{1,0:T(8,128)(2,1)S(1)} %copy.63, bf16[64,64]{1,0:T(8,128)(2,1)S(1)} %copy.69), kind=kLoop, calls=%fused_computation.2 | loop fusion | flops 524288 | bytes 1065088 | tf_op jit(solution)/shard_map/mul | solution.py:206
  37.3 13.6 %mul.185.wo_ref = bf16[512,512]{1,0:T(8,128)(2,1)} reshape(bf16[64,8,64,8]{3,2,1,0:T(8,128)(2,1)} %get-tuple-element.102) | data formatting | bytes 1048576 | tf_op jit(solution)/shard_map/mul | solution.py:206
  50.9 13.6 %mul.188.wot_ref = bf16[512,512]{1,0:T(8,128)(2,1)} reshape(bf16[64,8,64,8]{3,2,1,0:T(8,128)(2,1)} %get-tuple-element.101) | data formatting | bytes 1048576 | tf_op jit(solution)/shard_map/mul | solution.py:206
  64.7 0.7 broadcast_in_dim.24.sc_ref.refs_6_
  65.4 0.7 broadcast_in_dim.25.off_ref.refs_7_
  66.1 1.0 broadcast_in_dim.22.bias_ref
  67.1 0.8 broadcast_in_dim.23.gbias_ref
  68.0 16.0 %own_rows.1 = (bf16[64,64,512]{2,1,0:T(8,128)(2,1)}, f32[64,64,512]{2,1,0:T(8,128)}, bf16[64,64,512]{2,1,0:T(8,128)(2,1)}) custom-call(bf16[64,64,512]{2,1,0:T(8,128)(2,1)} %bitcast.38, bf16[64,64,512]{2,1,0:T(8,128)(2,1)} %bitcast.49, s32[64,512]{1,0:T(8,128)} %mask_ref.3, bf16[1024,512]{1,0:T(8,128)(2,1)} %mul.164.wk_ref, ...), custom_call_target="tpu_custom_call" | custom-call | flops 10000000000 | bytes 31457280 | tf_op jit(solution)/shard_map/own_rows/pallas_call | solution.py:262
  84.0 1.9 slice_bitcast_fusion.refs_1_
  85.8 0.8 broadcast_in_dim.26.refs_4_
  86.7 1.0 broadcast_in_dim.27.refs_5_
  87.7 22.4 %all_rows_0.1 = (bf16[32,512,512]{2,1,0:T(8,128)(2,1)}, bf16[64,512,512]{2,1,0:T(8,128)(2,1)}) custom-call(bf16[8,17,64,512]{3,2,1,0:T(8,128)(2,1)} %bitcast.45, bf16[8,64,512]{2,1,0:T(8,128)(2,1)} %slice_bitcast_fusion.refs_1_, bf16[512,512]{1,0:T(8,128)(2,1)} %mul.176.refs_2_, bf16[1024,512]{1,0:T(8,128)(2,1)} %mul.180.refs_3_, ...), custom_call_target="tpu_custom_call" | custom-call | flops 20000000000 | bytes 31457280 | tf_op jit(solution)/shard_map/all_rows_0/pallas_call | solution.py:280
  110.5 22.6 %all_rows_1.1 = (bf16[32,512,512]{2,1,0:T(8,128)(2,1)}, bf16[64,512,512]{2,1,0:T(8,128)(2,1)}) custom-call(bf16[8,16,64,512]{3,2,1,0:T(8,128)(2,1)} %bitcast.48, bf16[8,64,512]{2,1,0:T(8,128)(2,1)} %slice_bitcast_fusion.refs_1_, bf16[512,512]{1,0:T(8,128)(2,1)} %mul.176.refs_2_, ...), custom_call_target="tpu_custom_call", output_to_operand_aliasing={{0}: (8, {}), {1}: (9, {})} | custom-call | flops 20000000000 | bytes 31457280 | tf_op jit(solution)/shard_map/all_rows_1/pallas_call | solution.py:280
  133.1 24.8 %all-gather.13.cloned.1.call-done = bf16[128,64,512]{2,1,0:T(8,128)(2,1)} async-done(((bf16[16,64,512]{2,1,0:T(8,128)(2,1)}), bf16[128,64,512]{2,1,0:T(8,128)(2,1)}) %all-gather.13.cloned.1.call-update) | async-done | bytes 8388624 | tf_op jit(solution)/shard_map/all_gather | solution.py:255
  157.8 22.4 %all_rows_2.1 = (bf16[32,512,512]{2,1,0:T(8,128)(2,1)}, bf16[64,512,512]{2,1,0:T(8,128)(2,1)}) custom-call(bf16[8,16,64,512]{3,2,1,0:T(8,128)(2,1)} %bitcast.46, bf16[8,64,512]{2,1,0:T(8,128)(2,1)} %slice_bitcast_fusion.refs_1_, bf16[512,512]{1,0:T(8,128)(2,1)} %mul.176.refs_2_, ...), custom_call_target="tpu_custom_call", output_to_operand_aliasing={{0}: (8, {}), {1}: (9, {})} | custom-call | flops 20000000000 | bytes 31457280 | tf_op jit(solution)/shard_map/all_rows_2/pallas_call | solution.py:280
  180.2 24.8 %all-gather.9.cloned.1.call-done = bf16[128,64,512]{2,1,0:T(8,128)(2,1)} async-done(((bf16[16,64,512]{2,1,0:T(8,128)(2,1)}), bf16[128,64,512]{2,1,0:T(8,128)(2,1)}) %all-gather.9.cloned.1.call-update) | async-done | bytes 8388624 | tf_op jit(solution)/shard_map/all_gather | solution.py:255
  205.0 22.4 %all_rows_3.1 = (bf16[32,512,512]{2,1,0:T(8,128)(2,1)}, bf16[64,512,512]{2,1,0:T(8,128)(2,1)}) custom-call(bf16[8,16,64,512]{3,2,1,0:T(8,128)(2,1)} %bitcast.47, bf16[8,64,512]{2,1,0:T(8,128)(2,1)} %slice_bitcast_fusion.refs_1_, bf16[512,512]{1,0:T(8,128)(2,1)} %mul.176.refs_2_, ...), custom_call_target="tpu_custom_call", output_to_operand_aliasing={{0}: (8, {}), {1}: (9, {})} | custom-call | flops 20000000000 | bytes 31457280 | tf_op jit(solution)/shard_map/all_rows_3/pallas_call | solution.py:280
  227.4 0.8 broadcast_in_dim.28.bout_ref
  228.3 0.8 broadcast_in_dim.29.sc_ref
  229.1 0.9 broadcast_in_dim.30.off_ref
  230.0 65.7 %chain.1 = (bf16[4,64,64,128]{3,2,1,0:T(8,128)(2,1)}, bf16[64,64,512]{2,1,0:T(8,128)(2,1)}, bf16[64,64,512]{2,1,0:T(8,128)(2,1)}, f32[512,512]{1,0:T(8,128)}, f3...) custom-call(bf16[64,64,512]{2,1,0:T(8,128)(2,1)} %get-tuple-element.35.a_ref, ...), custom_call_target="tpu_custom_call" | custom-call | flops 20000000000 | bytes 62914560 | tf_op jit(solution)/shard_map/chain/pallas_call | solution.py:296
  295.7 4.9 %all-to-all-start = ((bf16[8,32,64,128]{3,2,1,0:T(8,128)(2,1)}), bf16[8,32,64,128]{3,2,1,0:T(8,128)(2,1)}, u32[]{:S(2)}, u32[]{:S(2)}) async-start(bf16[8,32,64,128]{3,2,1,0:T(8,128)(2,1)} %bitcast.40), calls=%async_computation | async-start | bytes 8388608 | tf_op jit(solution)/shard_map/all_to_all | solution.py:308
  300.6 49.4 %all-to-all-done.do_ref = bf16[8,32,64,128]{3,2,1,0:T(8,128)(2,1)} async-done(((bf16[8,32,64,128]{3,2,1,0:T(8,128)(2,1)}), bf16[8,32,64,128]{3,2,1,0:T(8,128)(2,1)}, u32[]{:S(2)}, u32[]{:S(2)}) %all-to-all-start) | async-done | bytes 4194336 | tf_op jit(solution)/shard_map/all_to_all | solution.py:308
  350.1 11.9 %db.1 = bf16[32,128,512]{2,1,0:T(8,128)(2,1)} custom-call(bf16[8,32,64,128]{3,2,1,0:T(8,128)(2,1)} %all-to-all-done.do_ref, bf16[32,512,512]{2,1,0:T(8,128)(2,1)} %get-tuple-element.47.a_ref), custom_call_target="tpu_custom_call" | custom-call | flops 10000000000 | bytes 31457280 | tf_op jit(solution)/shard_map/db/pallas_call | solution.py:310
  362.0 3.2 constant_dynamic-slice_fusion
  365.3 2.7 broadcast_multiply_fusion.2
  368.0 6.7 %mul.194 = bf16[512,2560]{0,1:T(8,128)(2,1)S(1)} reshape(bf16[8,64,320,8]{1,0,3,2:T(8,128)(2,1)} %broadcast_multiply_fusion.2) | data formatting | bytes 5242880 | tf_op jit(solution)/shard_map/mul | solution.py:326
  374.7 2.8 copy.72.wg_ref
  377.6 2.2 pad_maximum_fusion.3.bias_ref
  379.7 3.0 pad_maximum_fusion.1.wk_ref
  382.8 11.1 %reshape.163 = f32[64,8,64,8]{3,2,1,0:T(8,128)} reshape(f32[512,512]{1,0:T(8,128)S(1)} %copy-done.1) | data formatting | bytes 2097152 | tf_op jit(solution)/shard_map/reshape | solution.py:341
  396.1 7.5 %select_reduce_fusion = f32[64,64]{1,0:T(8,128)S(1)} fusion(f32[64,8,64,8]{3,2,1,0:T(8,128)} %reshape.163, pred[8,8]{1,0:T(8,128)(4,1)S(1)} %iota_compare_fusion.1), kind=kLoop, calls=%fused_computation | loop fusion | flops 520192 | bytes 1065024 | tf_op jit(solution)/shard_map/cidi->cd/reduce_sum | solution.py:341
  403.6 3.4 broadcast_select_fusion.1
  407.0 2.3 pad_maximum_fusion.db_ref
  409.4 41.7 %input_side.1 = (bf16[64,64,512]{2,1,0:T(8,128)(2,1)}, f32[64,2560]{1,0:T(8,128)}, f32[256,8,128]{2,1,0:T(8,128)}, f32[64,512]{1,0:T(8,128)}, f32[64,512]{1,0:T(8,128)}) custom-call(bf16[64,64,512]{2,1,0:T(8,128)(2,1)} %bitcast.39, bf16[64,64,512]{2,1,0:T(8,128)(2,1)} %bitcast.50, s32[64,512]{1,0:T(8,128)} %mask_ref.3, ...), custom_call_target="tpu_custom_call" | custom-call | flops 10000000000 | bytes 31457280 | tf_op jit(solution)/shard_map/input_side/pallas_call | solution.py:330
  451.1 1.6 copy.73
  453.1 1.0 reduce_sum.84
  454.4 27.8 %all-reduce = (bf16[64]{0:T(256)(128)(2,1)}, bf16[64]{0:T(256)(128)(2,1)}, bf16[64,256]{0,1:T(8,128)(2,1)S(1)}, bf16[256]{0:T(256)(128)(2,1)}, bf16[64]{0:T(256)...) all-reduce(f32[64]{0:T(128)S(1)} %reduce_sum.81, ...), channel_id=1, replica_groups=mesh['batch'=2,'dap'=8] {'dap'}, use_global_device_ids=true, to_apply=%region_1.2 | all-reduce | flops 25216 | bytes 151296 | tf_op jit(solution)/shard_map/psum | solution.py:344
  (84 shorter events, 7.8 us)
Async XLA Ops:
  7.2 76.8 %all-gather.11.cloned.1.call-start = ((), (), s32[]{:S(2)}) async-start(), calls=%async_computation.2 | async-start | bytes 10027008 | tf_op jit(solution)/shard_map/all_gather | solution.py:255
  7.3 4.0 copy-start.8
  11.2 3.6 copy-start.3
  11.2 4.0 copy-start.11
  12.5 5.5 %copy-start.13 = (bf16[256]{0:T(256)(128)(2,1)S(1)}, bf16[256]{0:T(256)(128)(2,1)}, u32[]{:S(2)}) copy-start(bf16[256]{0:T(256)(128)(2,1)} %param.19) | copy-start | bytes 1540
  12.5 98.0 %all-gather.15.cloned.1.call-start = ((), (), s32[]{:S(2)}) async-start(), calls=%async_computation.4 | async-start | bytes 9437184 | tf_op jit(solution)/shard_map/all_gather | solution.py:255
  13.3 144.5 %all-gather.13.cloned.1.call-start = ((), (), s32[]{:S(2)}) async-start(), calls=%async_computation.3 | async-start | bytes 9437184 | tf_op jit(solution)/shard_map/all_gather | solution.py:255
  14.1 190.8 %all-gather.9.cloned.1.call-start = ((), (), s32[]{:S(2)}) async-start(), calls=%async_computation.1 | async-start | bytes 9437184 | tf_op jit(solution)/shard_map/all_gather | solution.py:255
  20.3 10.6 %copy-start.12 = (bf16[64,64]{1,0:T(8,128)(2,1)S(1)}, bf16[64,64]{1,0:T(8,128)(2,1)}, u32[]{:S(2)}) copy-start(bf16[64,64]{1,0:T(8,128)(2,1)} %param.22) | copy-start | bytes 24580
  50.9 13.8 %copy-start.14 = (bf16[64]{0:T(256)(128)(2,1)S(1)}, bf16[64]{0:T(256)(128)(2,1)}, u32[]{:S(2)}) copy-start(bf16[64]{0:T(256)(128)(2,1)} %param.16) | copy-start | bytes 388
  50.9 14.5 %copy-start.15 = (bf16[64]{0:T(256)(128)(2,1)S(1)}, bf16[64]{0:T(256)(128)(2,1)}, u32[]{:S(2)}) copy-start(bf16[64]{0:T(256)(128)(2,1)} %param.17) | copy-start | bytes 388
  50.9 16.3 %copy-start.16 = (bf16[64]{0:T(256)(128)(2,1)S(1)}, bf16[64]{0:T(256)(128)(2,1)}, u32[]{:S(2)}) copy-start(bf16[64]{0:T(256)(128)(2,1)} %param.25) | copy-start | bytes 388
  205.0 22.5 %copy-start.17 = (bf16[64]{0:T(256)(128)(2,1)S(1)}, bf16[64]{0:T(256)(128)(2,1)}, u32[]{:S(2)}) copy-start(bf16[64]{0:T(256)(128)(2,1)} %param.23) | copy-start | bytes 388
  205.0 23.3 %copy-start.18 = (bf16[64]{0:T(256)(128)(2,1)S(1)}, bf16[64]{0:T(256)(128)(2,1)}, u32[]{:S(2)}) copy-start(bf16[64]{0:T(256)(128)(2,1)} %param.20) | copy-start | bytes 388
  205.0 24.2 %copy-start.19 = (bf16[64]{0:T(256)(128)(2,1)S(1)}, bf16[64]{0:T(256)(128)(2,1)}, u32[]{:S(2)}) copy-start(bf16[64]{0:T(256)(128)(2,1)} %param.21) | copy-start | bytes 388
  295.7 54.4 %all-to-all-start = ((bf16[8,32,64,128]{3,2,1,0:T(8,128)(2,1)}), bf16[8,32,64,128]{3,2,1,0:T(8,128)(2,1)}, u32[]{:S(2)}, u32[]{:S(2)}) async-start(bf16[8,32,64,128]{3,2,1,0:T(8,128)(2,1)} %bitcast.40), calls=%async_computation | async-start | bytes 8388608 | tf_op jit(solution)/shard_map/all_to_all | solution.py:308
  365.1 38.5 %collective-permute-start = (bf16[32,64,512]{2,1,0:T(8,128)(2,1)}, bf16[32,64,512]{2,1,0:T(8,128)(2,1)}, u32[]{:S(2)}, u32[]{:S(2)}) collective-permute-start(bf16[32,64,512]{2,1,0:T(8,128)(2,1)} %constant_dynamic-slice_fusion), channel_id=1, source_target_pairs={{0,1},{1,0},{2,3},{3,2},{4,5},{5,4},{6,7},{7,6},{8,9},{9,8},{10,11... | collective-permute-start | bytes 6291464 | tf_op jit(solution)/shard_map/ppermute | solution.py:320
  374.7 2.8 copy-start
  377.5 5.2 %copy-start.1 = (f32[512,512]{1,0:T(8,128)S(1)}, f32[512,512]{1,0:T(8,128)}, u32[]{:S(2)}) copy-start(f32[512,512]{1,0:T(8,128)} %get-tuple-element.56) | copy-start | bytes 3145732
  382.8 11.2 %copy-start.7 = (f32[64,8,128]{2,1,0:T(8,128)S(1)}, f32[64,8,128]{2,1,0:T(8,128)}, u32[]{:S(2)}) copy-start(f32[64,8,128]{2,1,0:T(8,128)} %get-tuple-element.54) | copy-start | bytes 786436
  382.8 11.7 %copy-start.6 = (f32[64,8,128]{2,1,0:T(8,128)S(1)}, f32[64,8,128]{2,1,0:T(8,128)}, u32[]{:S(2)}) copy-start(f32[64,8,128]{2,1,0:T(8,128)} %get-tuple-element.55) | copy-start | bytes 786436
  382.8 12.3 %copy-start.5 = (f32[64,8,128]{2,1,0:T(8,128)S(1)}, f32[64,8,128]{2,1,0:T(8,128)}, u32[]{:S(2)}) copy-start(f32[64,8,128]{2,1,0:T(8,128)} %get-tuple-element.57) | copy-start | bytes 786436
  382.8 12.8 %copy-start.4 = (f32[64,8,128]{2,1,0:T(8,128)S(1)}, f32[64,8,128]{2,1,0:T(8,128)}, u32[]{:S(2)}) copy-start(f32[64,8,128]{2,1,0:T(8,128)} %get-tuple-element.58) | copy-start | bytes 786436
  451.1 2.0 copy-start.2
  451.1 3.1 copy-start.10
  451.1 3.2 copy-start.9
Sparse Core Ops, SparseCore 0:
  12.6 50.5 all-gather.10
  64.8 45.6 all-gather.14
  112.1 45.6 all-gather.12
  159.3 45.6 all-gather.8

commit v2 on v0

v2 whole, which is shorter than its diff:
```python
import functools
import jax
import jax.numpy as jnp
from jax import lax
from jax.experimental import pallas as pl
from jax.experimental.pallas import tpu as pltpu
from jax.sharding import PartitionSpec as P

LN_EPS = 1e-5
F32 = jnp.float32
BF16 = jnp.bfloat16
SUB = 8
VMEM_LIMIT = 63 * 1024 * 1024
COST = 5e8


def nn_dot(lhs, rhs):
    return lax.dot_general(lhs, rhs, (((1,), (0,)), ((), ())), preferred_element_type=F32)


def nt_dot(lhs, rhs):
    return lax.dot_general(lhs, rhs, (((1,), (1,)), ((), ())), preferred_element_type=F32)


def tn_dot(lhs, rhs):
    return lax.dot_general(lhs, rhs, (((0,), (0,)), ((), ())), preferred_element_type=F32)


def row_norm(z8, scale, offset):
    mean_val = jnp.mean(z8, axis=1, keepdims=True)
    centered = z8 - mean_val
    inv_std = lax.rsqrt(jnp.mean(centered * centered, axis=1, keepdims=True) + LN_EPS)
    z_hat = centered * inv_std
    return z_hat, inv_std, (z_hat * scale[None] + offset[None]).astype(BF16)


def lanes(bias, width):
    return jnp.concatenate([bias] * (width // bias.shape[-1]), axis=-1)


def gated(prod, bias_ref, start, chans, mask_half):
    cols = prod.shape[-1]
    val = prod[:chans * SUB].reshape(chans, SUB, cols) + lanes(bias_ref[start:start + chans], cols)
    gate = prod[chans * SUB:].reshape(chans, SUB, cols) + lanes(bias_ref[start + chans:start + 2 * chans], cols)
    return (jnp.tanh(gate) + 1.0) * (val * mask_half[None])


def build_weights(core, w_in, w_out, w_gate, vecs, wk_ref, wg_ref, bias_ref, sc_ref, off_ref, perm_s, wok_s, wotk_s, bo_s, osc_s, ooff_s):
    cz = w_in.shape[0]
    ch = w_in.shape[1] // 4
    big = ch * SUB

    def iota(shape, dim):
        return lax.broadcasted_iota(jnp.int32, shape, dim)

    def one(cond):
        return jnp.where(cond, 1.0, 0.0).astype(BF16)

    turn = core * (ch // 2)
    rep = iota((big, ch), 0) // SUB == iota((big, ch), 1)
    rep_c = lax.rem(iota((big, ch), 0) // SUB + turn, ch) == iota((big, ch), 1)
    rep_t = iota((ch, big), 1) // SUB == iota((ch, big), 0)
    rep_ct = lax.rem(iota((ch, big), 1) // SUB + turn, ch) == iota((ch, big), 0)
    tile = one(iota((cz, SUB * cz), 1) % cz == iota((cz, SUB * cz), 0))
    tile_t = one(iota((SUB * cz, cz), 0) % cz == iota((SUB * cz, cz), 1))
    keep = iota((big, SUB * cz), 0) % SUB == iota((big, SUB * cz), 1) // cz
    keep_t = iota((SUB * cz, big), 1) % SUB == iota((SUB * cz, big), 0) // cz
    same = iota((big, big), 0) % SUB == iota((big, big), 1) % SUB

    def spread(wide):
        return jnp.where(keep, nn_dot(wide, tile), 0.0).astype(BF16)

    def column(sel, row, width):
        picked = jnp.where(sel, jnp.broadcast_to(row.astype(F32), sel.shape), 0.0).astype(BF16)
        return nn_dot(picked, jnp.ones((sel.shape[1], width), BF16))

    def eights(sel, row):
        return column(sel, row, 128).reshape(ch, SUB, 128)

    for dst, src, scale in ((0, 0, 1.0), (1, 2, 0.5), (2, 1, 1.0), (3, 3, 0.5), (4, None, 1.0)):
        w_part = w_gate[...] if src is None else w_in[:, src * ch:(src + 1) * ch]
        sel, sel_t = (rep, rep_t) if src is None else (rep_c, rep_ct)
        at = slice(dst * big, (dst + 1) * big)
        wide = (nt_dot(one(sel), w_part) * scale).astype(BF16)
        wk_ref[at] = spread(wide)
        wg_ref[:, at] = jnp.where(keep_t, nn_dot(tile_t, nn_dot(w_part, one(sel_t)).astype(BF16)), 0.0).astype(BF16)
        vec = 5 if src is None else 6 + src
        bias_ref[dst * ch:(dst + 1) * ch] = eights(sel, vecs[vec:vec + 1]) * scale
    eye = iota((cz, cz), 0) == iota((cz, cz), 1)
    perm_s[...] = spread(one(rep))
    wok_s[...] = jnp.where(same, nn_dot(nt_dot(one(rep), w_out[...]).astype(BF16), one(rep_ct)), 0.0).astype(BF16)
    wotk_s[...] = jnp.where(same, nn_dot(nn_dot(one(rep_c), w_out[...]).astype(BF16), one(rep_t)), 0.0).astype(BF16)
    sc_ref[...] = column(eye, vecs[0:1], sc_ref.shape[1])
    off_ref[...] = column(eye, vecs[1:2], off_ref.shape[1])
    osc_s[...] = eights(rep_c, vecs[2:3])
    ooff_s[...] = eights(rep_c, vecs[3:4])
    bo_s[...] = eights(rep, vecs[4:5])


def project(z8, mask_half, wk_ref, bias_ref, sc_ref, off_ref, chans):
    cols = z8.shape[-1]
    _, _, zn = row_norm(z8.astype(F32), sc_ref[...], off_ref[...])
    zn2 = zn.reshape(SUB * zn.shape[1], cols)
    n_p = 2 * chans * SUB
    act_a = gated(nn_dot(wk_ref[:n_p], zn2), bias_ref, 0, chans, mask_half)
    act_b = gated(nn_dot(wk_ref[n_p:2 * n_p], zn2), bias_ref, 2 * chans, chans, mask_half)
    return act_a, act_b, zn2


MESH = pl.DeviceIdType.MESH
OWN, LEFT, RIGHT, OPP = range(4)
HOPS = (0, -1, 1, 2)


def blk(shape, index_map):
    return pl.BlockSpec(shape, index_map)


def front_kernel(n_dap, z_own, dy_ref, m_own, w_in, w_out, w_gate, vecs,
                 da_ref, keep_ref, got_ref, dgl_ref, gram_ref, dbg_ref, dbo_ref, dsc_ref, dof_ref, wk_ref, wg_ref, bias_ref, sc_ref, off_ref,
                 give_ref, z_far, m_far, a_all, b_pair, a_sib, lg_ref, dyt_ref, do_out, do_in,
                 perm_ref, wo_ref, wot_ref, bout_ref, osc_ref, ooff_ref,
                 o_s, gram_s, lg_v, dyt_v, do_v, dgl_v, send_sem, recv_sem, loc_sem):
    n_chip = n_dap // 2
    _, rows, cz, cols = z_own.shape
    z_ref, mask_ref = z_own.at[0], m_own.at[0]
    chans = a_all.shape[1]
    half = chans // 2
    hr = rows // 2
    jb = 2 * rows
    grp = 2 * SUB
    me = lax.axis_index('dap')
    core, chip = lax.rem(me, 2), me // 2
    low = core == 0

    def peer(hop, flip):
        to = lax.rem(chip + (hop + n_chip), n_chip) * 2
        return {'dap': to + (1 - core if flip else core)}

    def copy(k, src, dst, hop, flip):
        return pltpu.make_async_remote_copy(src_ref=src, dst_ref=dst, send_sem=send_sem.at[k], recv_sem=recv_sem.at[k],
                                            device_id=peer(hop, flip), device_id_type=MESH)

    barrier = pltpu.get_barrier_semaphore()
    for hop in HOPS:
        for flip in (0, 1):
            if hop or flip:
                pl.semaphore_signal(barrier, inc=1, device_id=peer(hop, flip), device_id_type=MESH)
    pl.semaphore_wait(barrier, n_dap - 1)

    n_grp = rows // grp
    masks = [copy(i, mask_ref, m_far.at[i], hop, 0) for i, hop in enumerate((1, -1, 2))]
    quarter = lambda q: pl.ds(pl.multiple_of(q * grp, grp), grp)
    z_r = lambda q: copy(3 + q, z_ref.at[quarter(q)], z_far.at[0, quarter(q)], 1, 0)
    z_l = lambda q: copy(3 + n_grp + q, z_ref.at[quarter(q)], z_far.at[1, quarter(q)], -1, 0)
    fwd_r = lambda q: copy(3 + 2 * n_grp + q, z_far.at[0, quarter(q)], z_far.at[2, quarter(q)], 1, 0)
    fwd_l = lambda q: copy(3 + 2 * n_grp + q, z_far.at[1, quarter(q)], z_far.at[2, quarter(q)], -1, 0)
    base_b = 3 + 3 * n_grp
    my_rows = pl.multiple_of(core * rows, rows)

    def swap_b(r, q):
        at = pl.ds(pl.multiple_of(my_rows + q * grp, grp), grp)
        return [copy(base_b + (r * n_grp + q) * 2 + h, b_pair.at[r, pl.ds(h * half, half), at], b_pair.at[r, pl.ds((1 - h) * half, half), at], 0, 1) for h in (0, 1)]

    base_a = base_b + 8 * n_grp
    swap_a = lambda r, q: copy(base_a + r * n_grp + q, a_all.at[r, pl.ds(half, half), quarter(q)], a_sib.at[r, :, quarter(q)], 0, 1)
    base_s = base_a + 4 * n_grp
    back = (OWN, RIGHT, LEFT, OPP)
    ship = [[None if (r == OWN and side == 0) else
             copy(base_s + 2 * r + side, do_out.at[r, pl.ds(side * half, half)], do_in.at[back[r], side], HOPS[r], side) for side in (0, 1)] for r in range(4)]
    swap_d = [copy(base_s + 8 + q, give_ref.at[pl.ds(q * (half // 2), half // 2)], got_ref.at[pl.ds(q * (half // 2), half // 2)], 0, 1) for q in (0, 1)]

    for c in masks:
        c.start()
    for q in range(n_grp):
        z_r(q).start()
        z_l(n_grp - 1 - q).start()
    build_weights(core, w_in, w_out, w_gate, vecs, wk_ref, wg_ref, bias_ref, sc_ref, off_ref, perm_ref, wo_ref, wot_ref, bout_ref, osc_ref, ooff_ref)

    row3 = blk((grp, cz, cols), lambda g: (g, 0, 0))
    row2 = blk((grp, cols), lambda g: (g, 0))
    chan3 = lambda n: blk((n, grp, cols), lambda g: (0, g, 0))

    def ab_body(z_b, m_b, a_b, b_b):
        a_parts, b_parts = [], []
        for h in range(2):
            rws = slice(h * SUB, (h + 1) * SUB)
            act_a, act_b, _ = project(z_b[0, rws], m_b[0, rws].astype(F32) * 0.5, wk_ref, bias_ref, sc_ref, off_ref, chans)
            a_parts.append(act_a)
            b_parts.append(act_b)
        a_b[0] = jnp.concatenate(a_parts, axis=1).astype(BF16)
        b_b[0] = jnp.concatenate(b_parts, axis=1).astype(BF16)

    def project_rows(z_src, m_src, n, slot, place):
        pltpu.emit_pipeline(
            ab_body, grid=(n,),
            in_specs=[blk((1, grp, cz, cols), lambda g: (slot(g), place(g)[1], 0, 0)), blk((1, grp, cols), lambda g: (slot(g), place(g)[1], 0))],
            out_specs=[blk((1, chans, grp, cols), lambda g: (place(g)[0], 0, place(g)[1], 0)),
                       blk((1, chans, grp, cols), lambda g: (place(g)[0], 0, core * n_grp + place(g)[1], 0))])(z_src, m_src, a_all, b_pair)

    def swap(r, q):
        for c in swap_b(r, q):
            c.start()
        swap_a(r, q).start()

    def swapped_b(r):
        def body(q, carry):
            for c in swap_b(r, q):
                c.wait_recv()
            return carry
        lax.fori_loop(0, n_grp, body, 0)

    def lg_body(z_b, dy_b, lg_b, dyt_b):
        dy_parts = []
        for h in range(2):
            rws = slice(h * SUB, (h + 1) * SUB)
            _, _, zn = row_norm(z_b[rws].astype(F32), sc_ref[...], off_ref[...])
            zn2 = zn.reshape(SUB * cz, cols)
            lg_b[:, rws, :] = nn_dot(wk_ref[4 * chans * SUB:], zn2).reshape(cz, SUB, cols) + lanes(bias_ref[4 * chans:], cols)
            dy_parts.append(nn_dot(perm_ref[...], dy_b[rws].reshape(SUB * cz, cols)).reshape(cz, SUB, cols))
        dyt_b[...] = jnp.concatenate(dy_parts, axis=1).astype(BF16)

    for ref in (dbg_ref, dbo_ref, dsc_ref, dof_ref, gram_s):
        ref[...] = jnp.zeros_like(ref)

    per = chans // 8

    def o_body(a_b, b_b):
        base = pl.program_id(0) * per
        for c in range(per):
            o_s[base + c] = nt_dot(a_b[c], b_b[c])

    def chain(r):
        where = lax.rem(chip + (HOPS[r] + n_chip), n_chip)
        col = pl.ds(pl.multiple_of(where * jb, jb), jb)
        get_lg = pltpu.make_async_copy(lg_ref.at[:, :, col], lg_v, loc_sem.at[0])
        get_dy = pltpu.make_async_copy(dyt_ref.at[:, :, col], dyt_v, loc_sem.at[1])
        get_lg.start()
        get_dy.start()
        pltpu.emit_pipeline(o_body, grid=(8,), in_specs=[blk((per, rows, cols), lambda s: (s, 0, 0)), blk((per, jb, cols), lambda s: (s, 0, 0))])(
            a_all.at[OWN], b_pair.at[r])
        get_lg.wait()
        get_dy.wait()

        def chain_body(g, carry):
            pair = pl.ds(pl.multiple_of(g * 2 * SUB, 2 * SUB), 2 * SUB)

            def wide(ref):
                val = ref[:, pair, :].astype(F32)
                return jnp.concatenate([val[:, :SUB], val[:, SUB:]], axis=2)

            def tall(val):
                return jnp.concatenate([val[..., :jb], val[..., jb:]], axis=1)

            def add(ref, val):
                ref[...] += val[..., :jb] + val[..., jb:]

            twice = lambda ref: lanes(ref[...], 2 * jb)
            o8 = wide(o_s)
            centered = o8 - jnp.mean(o8, axis=0, keepdims=True)
            inv_std = lax.rsqrt(jnp.mean(centered * centered, axis=0, keepdims=True) + LN_EPS)
            o_hat = centered * inv_std
            o_norm = (o_hat * twice(osc_ref) + twice(ooff_ref)).astype(BF16).reshape(chans * SUB, 2 * jb)
            upd = (nn_dot(wo_ref[...], o_norm).reshape(cz, SUB, 2 * jb) + twice(bout_ref)).astype(BF16).astype(F32)
            sig = jnp.tanh(wide(lg_v) * 0.5) * 0.5 + 0.5
            prod = sig * wide(dyt_v)
            d_upd = prod.astype(BF16)
            dgl = prod * upd * (1.0 - sig)
            add(dbg_ref, dgl)
            dgl_v[:, pair, :] = tall(dgl).astype(BF16)
            add(dbo_ref, d_upd.astype(F32))
            d_upd2 = d_upd.reshape(cz * SUB, 2 * jb)
            gram_s[...] += nt_dot(o_norm, d_upd2)
            d_on = nn_dot(wot_ref[...], d_upd2).astype(BF16).astype(F32).reshape(chans, SUB, 2 * jb)
            add(dsc_ref, d_on * o_hat)
            add(dof_ref, d_on)
            g_hat = d_on * twice(osc_ref)
            m1 = jnp.mean(g_hat, axis=0, keepdims=True)
            m2 = jnp.mean(g_hat * o_hat, axis=0, keepdims=True)
            do_v[:, pair, :] = tall(inv_std * (g_hat - m1 - o_hat * m2)).astype(BF16)
            return carry
        lax.fori_loop(0, rows // (2 * SUB), chain_body, 0)
        put_do = pltpu.make_async_copy(do_v, do_out.at[r], loc_sem.at[0])
        put_gl = pltpu.make_async_copy(dgl_v, dgl_ref.at[:, :, col], loc_sem.at[1])
        put_do.start()
        put_gl.start()
        put_do.wait()
        put_gl.wait()
        for c in ship[r]:
            if c is not None:
                c.start()

    project_rows(z_own, m_own, n_grp, lambda g: 0, lambda g: (OWN, g))
    for q in range(n_grp):
        swap(OWN, q)
    pltpu.emit_pipeline(lg_body, grid=(n_grp,), in_specs=[row3, row3], out_specs=[chan3(cz), chan3(cz)])(z_own.at[0], dy_ref, lg_ref, dyt_ref)
    swapped_b(OWN)
    chain(OWN)
    for c in masks:
        c.wait_recv()

    def sides(t, carry):
        z_r(t).wait_recv()
        z_l(n_grp - 1 - t).wait_recv()

        @pl.when(t < n_grp // 2)
        def _():
            fwd_r(t).start()
            fwd_l(n_grp - 1 - t).start()
        project_rows(z_far, m_far, 2, lambda g: g, lambda g: (g + LEFT, jnp.where(g == 0, t, n_grp - 1 - t)))
        swap(LEFT, t)
        swap(RIGHT, n_grp - 1 - t)
        return carry
    lax.fori_loop(0, n_grp, sides, 0)
    swapped_b(LEFT)
    chain(LEFT)
    swapped_b(RIGHT)
    chain(RIGHT)

    def opposite(t, carry):
        fwd_r(t).wait_recv()
        fwd_l(n_grp - 1 - t).wait_recv()
        project_rows(z_far, m_far, 2, lambda g: 2, lambda g: (OPP, jnp.where(g == 0, t, n_grp - 1 - t)))
        swap(OPP, t)
        swap(OPP, n_grp - 1 - t)
        return carry
    lax.fori_loop(0, n_grp // 2, opposite, 0)
    swapped_b(OPP)
    chain(OPP)

    gram = gram_s[...]
    n = gram.shape[0]
    diag = lax.broadcasted_iota(jnp.int32, (n, n), 0) % SUB == lax.broadcasted_iota(jnp.int32, (n, n), 1) % SUB
    gram_ref[...] = jnp.sum(jnp.where(diag, gram, 0.0).reshape(chans, SUB, n), axis=1)

    pc = 4
    n_a = chans // pc

    def da_body(do_b, b_b, da_b):
        for c in range(pc):
            lhs = jnp.concatenate([do_b[r, c] for r in range(4)], axis=1)
            rhs = jnp.concatenate([b_b[r, c] for r in range(4)], axis=0)
            da_b[c] = nn_dot(lhs, rhs).astype(BF16)

    pltpu.emit_pipeline(
        da_body, grid=(n_a,),
        in_specs=[blk((4, pc, rows, jb), lambda s: (0, s, 0, 0)), blk((4, pc, jb, cols), lambda s: (0, s, 0, 0))],
        out_specs=[blk((pc, rows, cols), lambda s: (s, 0, 0))])(do_out, b_pair, da_ref)

    for r in range(4):
        lax.fori_loop(0, n_grp, lambda q, carry, r=r: (swap_a(r, q).wait_recv(), carry)[1], 0)
        for c in ship[r]:
            if c is not None:
                c.wait_recv()

    def db_body(own_b, do0_b, do1_b, am_b, as_b, keep_b, give_b):
        for c in range(pc):
            lhs, rhs = [], []
            for r in range(4):
                lhs += [own_b[0, c] if r == OWN else do0_b[r - 1, c], do1_b[r, 0, c]]
                rhs += [am_b[r, c], as_b[r, c]]
            pair = tn_dot(jnp.concatenate(lhs, axis=0), jnp.concatenate(rhs, axis=0)).astype(BF16)
            keep_b[c] = jnp.where(low, pair[:rows], pair[rows:])
            give_b[c] = jnp.where(low, pair[rows:], pair[:rows])

    for q in (0, 1):
        steps = half // pc // 2
        at = lambda s: s + q * steps
        c3 = blk((pc, rows, cols), lambda s: (at(s), 0, 0))
        pltpu.emit_pipeline(
            db_body, grid=(steps,),
            in_specs=[blk((1, pc, rows, jb), lambda s: (0, at(s), 0, 0)), blk((3, pc, rows, jb), lambda s: (0, at(s), 0, 0)),
                      blk((4, 1, pc, rows, jb), lambda s: (0, 0, at(s), 0, 0)),
                      c4_at(pc, rows, cols, at), c4_at(pc, rows, cols, at)],
            out_specs=[c3, c3])(do_out, do_in.at[pl.ds(1, 3), 0], do_in.at[:, pl.ds(1, 1)], a_all, a_sib, keep_ref, give_ref)
        swap_d[q].start()
    for c in swap_d:
        c.wait_recv()
    for c in masks + swap_d + [c for pair in ship for c in pair if c is not None]:
        c.wait_send()

    def sent(q, carry):
        z_r(q).wait_send()
        z_l(q).wait_send()
        for r in range(4):
            for c in swap_b(r, q) + [swap_a(r, q)]:
                c.wait_send()

        @pl.when(q < n_grp // 2)
        def _():
            fwd_r(q).wait_send()

        @pl.when(q >= n_grp // 2)
        def _():
            fwd_l(q).wait_send()
        return carry
    lax.fori_loop(0, n_grp, sent, 0)


def c4_at(pc, rows, cols, at):
    return pl.BlockSpec((4, pc, rows, cols), lambda s: (0, at(s), 0, 0))


def input_kernel(z_ref, dy_ref, mask_ref, da_ref, db0_ref, db1_ref, dgl_ref, wk_ref, bias_ref, wg_ref, sc_ref, off_ref,
                 dz_ref, gram_ref, dbias_ref, dsc_ref, dof_ref, dp_s):
    chans = da_ref.shape[0]
    chan_z, cols = z_ref.shape[1:]

    @pl.when(pl.program_id(0) == 0)
    def _():
        for ref in (gram_ref, dbias_ref, dsc_ref, dof_ref):
            ref[...] = jnp.zeros_like(ref)

    def fold(val):
        acc = val[..., :128]
        for lane in range(128, cols, 128):
            acc = acc + val[..., lane:lane + 128]
        return acc

    n_p = chans * SUB
    grads = (da_ref[...].astype(F32), jnp.concatenate([db0_ref[...], db1_ref[...]], axis=0).astype(F32))
    for half in range(2):
        rows = slice(half * SUB, (half + 1) * SUB)
        z_hat, inv_std, zn = row_norm(z_ref[rows].astype(F32), sc_ref[...], off_ref[...])
        zn2 = zn.reshape(SUB * chan_z, cols)
        mask_f = mask_ref[rows].astype(F32)[None]
        for side, grad_all in enumerate(grads):
            prod = nn_dot(wk_ref[side * 2 * n_p:(side + 1) * 2 * n_p], zn2)
            val = prod[:n_p].reshape(chans, SUB, cols) + lanes(bias_ref[side * 2 * chans:side * 2 * chans + chans], cols)
            gate = prod[n_p:].reshape(chans, SUB, cols) + lanes(bias_ref[side * 2 * chans + chans:(side + 1) * 2 * chans], cols)
            sig = jnp.tanh(gate) * 0.5 + 0.5
            grad = grad_all[:, rows] * mask_f
            d_val = grad * sig
            d_gate = d_val * val * (1.0 - sig)
            dbias_ref[2 * side * chans:(2 * side + 1) * chans] += fold(d_val)
            dbias_ref[(2 * side + 1) * chans:(2 * side + 2) * chans] += fold(d_gate)
            dp_s[2 * side * n_p:(2 * side + 1) * n_p] = d_val.astype(BF16).reshape(n_p, cols)
            dp_s[(2 * side + 1) * n_p:(2 * side + 2) * n_p] = d_gate.astype(BF16).reshape(n_p, cols)
        dp_s[4 * n_p:] = dgl_ref[...].astype(F32)[:, rows].astype(BF16).reshape(n_p, cols)
        d_zn = nn_dot(wg_ref[...], dp_s[...]).astype(BF16).astype(F32).reshape(SUB, chan_z, cols)
        gram = nt_dot(zn2, dp_s[...]).reshape(SUB, chan_z, dp_s.shape[0])
        lane_row = lax.broadcasted_iota(jnp.int32, (chan_z, dp_s.shape[0]), 1) % SUB
        acc = gram_ref[...]
        for i in range(SUB):
            acc = acc + jnp.where(lane_row == i, gram[i], 0.0)
        gram_ref[...] = acc
        dsc_ref[...] += jnp.sum(d_zn * z_hat, axis=0)
        dof_ref[...] += jnp.sum(d_zn, axis=0)
        g_hat = d_zn * sc_ref[...][None]
        m1 = jnp.mean(g_hat, axis=1, keepdims=True)
        m2 = jnp.mean(g_hat * z_hat, axis=1, keepdims=True)
        d_z = dy_ref[rows].astype(F32) + inv_std * (g_hat - m1 - z_hat * m2)
        dz_ref[rows] = d_z.astype(BF16)


def whole(arr):
    nd = arr.ndim
    return pl.BlockSpec(arr.shape, lambda *_: (0,) * nd, pipeline_mode=pl.Buffered(1))


def call(kernel, name, us, *args, **kw):
    cost = pl.CostEstimate(flops=int(us * COST), bytes_accessed=2**20, transcendentals=0)
    return pl.pallas_call(kernel, name=name, cost_estimate=cost, compiler_params=pltpu.CompilerParams(vmem_limit_bytes=VMEM_LIMIT), **kw)(*args)


def local_grads(n_dap, z_loc, mask_loc, dy_loc, ln_in_scale, ln_in_offset, w_in, b_in, ln_out_scale, ln_out_offset, w_out, b_out, w_gate, b_gate):
    rows, cols, cz = z_loc.shape
    ch = w_in.shape[1] // 4
    half = ch // 2
    jb = 2 * rows
    grp = 2 * SUB
    n_grp = rows // grp
    sds = jax.ShapeDtypeStruct
    me = lax.axis_index('dap')
    core = me % 2
    z_t = jnp.transpose(z_loc, (0, 2, 1))
    dy_t = jnp.transpose(dy_loc, (0, 2, 1))

    def order(arr):
        return jnp.where(core == 0, arr, jnp.roll(arr, half, axis=0))

    n_e = 5 * ch
    b16 = lambda *shape: sds(shape, BF16)
    vecs = jnp.concatenate([ln_in_scale, ln_in_offset, ln_out_scale, ln_out_offset, b_out, b_gate, b_in]).reshape(-1, cz)
    row3 = lambda nd: pl.BlockSpec((grp, nd, cols), lambda g: (g, 0, 0))
    chan_rows = lambda n: pl.BlockSpec((n, grp, cols), lambda g: (0, g, 0))
    mask_spec = pl.BlockSpec((grp, cols), lambda g: (g, 0))
    f32 = lambda *shape: sds(shape, F32)
    any_spec = pl.BlockSpec(memory_space=pl.ANY)
    vmem = pl.BlockSpec(memory_space=pltpu.VMEM)
    n_copy = 3 + 3 * n_grp + 8 * n_grp + 4 * n_grp + 10
    acc = f32(ch, SUB, 128)
    blocks = pltpu.VMEM((ch * SUB, cz * SUB), BF16)
    spread = pltpu.VMEM((ch, SUB, 128), F32)
    outs = pl.pallas_call(
        functools.partial(front_kernel, n_dap), name='front',
        out_shape=(b16(ch, rows, cols), b16(half, rows, cols), b16(half, rows, cols), b16(cz, rows, cols), f32(ch, cz * SUB), acc, acc, acc, acc,
                   b16(n_e * SUB, SUB * cz), b16(SUB * cz, n_e * SUB), f32(n_e, SUB, 128), f32(cz, cols), f32(cz, cols),
                   b16(half, rows, cols), b16(3, rows, cz, cols), sds((3, rows, cols), jnp.int32), b16(4, ch, rows, cols), b16(4, ch, jb, cols),
                   b16(4, half, rows, cols), f32(cz, rows, cols), b16(cz, rows, cols), b16(4, ch, rows, jb), b16(4, 2, half, rows, jb)),
        in_specs=[any_spec] * 3 + [vmem] * 4,
        out_specs=(any_spec,) * 4 + (vmem,) * 10 + (any_spec,) * 10,
        scratch_shapes=[blocks, blocks, blocks, spread, spread, spread,
                        pltpu.VMEM((ch, rows, jb), F32), pltpu.VMEM((ch * SUB, cz * SUB), F32), pltpu.VMEM((cz, rows, jb), F32),
                        pltpu.VMEM((cz, rows, jb), BF16), pltpu.VMEM((ch, rows, jb), BF16), pltpu.VMEM((cz, rows, jb), BF16),
                        pltpu.SemaphoreType.DMA((n_copy,)), pltpu.SemaphoreType.DMA((n_copy,)), pltpu.SemaphoreType.DMA((2,))],
        cost_estimate=pl.CostEstimate(flops=10**11, bytes_accessed=2**20, transcendentals=0),
        compiler_params=pltpu.CompilerParams(vmem_limit_bytes=VMEM_LIMIT, collective_id=0, has_side_effects=True),
    )(z_t[None], dy_t, mask_loc[None], w_in, w_out, w_gate, vecs)
    da, keep, got, dgl, gram_o, dbg, dbo, dsc_o, dof_o, wk, wg, bias, sc_in, off_in = outs[:14]

    args = (z_t, dy_t, mask_loc, da, keep, got, dgl, wk, bias, wg, sc_in, off_in)
    const = lambda *shape: pl.BlockSpec(shape, lambda g: (0,) * len(shape))
    dz_t, gram_i, dbias, dsc_i, dof_i = call(
        input_kernel, 'input_side', 42, *args, grid=(n_grp,),
        out_shape=(b16(rows, cz, cols), sds((cz, n_e * SUB), F32), sds((4 * ch, SUB, 128), F32), sds((cz, cols), F32), sds((cz, cols), F32)),
        in_specs=[row3(cz), row3(cz), mask_spec, chan_rows(ch), chan_rows(half), chan_rows(half), chan_rows(cz)] + [whole(x) for x in args[7:]],
        out_specs=(row3(cz), const(cz, n_e * SUB), const(4 * ch, SUB, 128), const(cz, cols), const(cz, cols)),
        scratch_shapes=[pltpu.VMEM((n_e * SUB, cols), BF16)])

    d_w = jnp.transpose(gram_i.reshape(cz, n_e, SUB).sum(-1))
    d_wout = gram_o.reshape(ch, cz, SUB).sum(-1)
    tail = lambda acc: acc.sum((-2, -1))
    dbias = tail(dbias)
    by_name = lambda arr: jnp.concatenate([order(arr[i * ch:(i + 1) * ch]) for i in (0, 2, 1, 3)])
    partial = (dsc_i.sum(-1), dof_i.sum(-1), by_name(d_w), by_name(dbias), order(tail(dsc_o)), order(tail(dof_o)), order(d_wout), tail(dbo), d_w[4 * ch:], tail(dbg))
    summed = [piece.astype(BF16) for piece in lax.psum(partial, 'dap')]
    summed[2] = summed[2].T
    summed[8] = summed[8].T
    return (jnp.transpose(dz_t, (0, 2, 1)),) + tuple(summed)


def solution(mesh):
    pair_spec = P(('batch', 'dap'), None, None)
    mask_spec = P(('batch', 'dap'), None)
    vec_rep = P(None)
    mat_rep = P(None, None)
    vec_part = P('batch')
    mat_part = P('batch', None)
    in_specs = (pair_spec, mask_spec, pair_spec, vec_rep, vec_rep, mat_rep, vec_rep, vec_rep, vec_rep, mat_rep, vec_rep, mat_rep, vec_rep)
    out_specs = (pair_spec, vec_part, vec_part, mat_part, vec_part, vec_part, vec_part, mat_part, vec_part, mat_part, vec_part)
    body = functools.partial(local_grads, mesh.shape['dap'])
    return jax.shard_map(body, mesh=mesh, in_specs=in_specs, out_specs=out_specs, check_vma=False)
```

time: 802 us -> 311 us (0.39)
  waiting for transfers between devices: 399 us -> 0 us
  Pallas kernels: 0 us -> 264 us
  matrix products: 192 us -> 0 us
  other arithmetic: 101 us -> 7.11 us
  local copies, waits for them, and re-layouts: 61.3 us -> 8.78 us
  between operations: 14.8 us -> 0.8 us
    reduce_scatter x1 -> x0, waiting for transfers between devices: 267 us -> none  [local_grads(): d_act_b = lax.psum_scatter(d_b_part, 'dap', scatter_dimension=1, tiled=True)]
    pallas_call x0 -> x2, Pallas kernels: none -> 264 us  [the longest x1 223 us: local_grads(): pl.pallas_call(functools.partial(front_kernel, n_dap), name='front', out_...]
    dot_general x12 -> x0, matrix products: 192 us -> none  [the longest x1 45.7 us: local_grads(): jnp.einsum('cik,cjk->cij', act_a, b_full, preferred_element_type=jnp.floa...]
    all_gather x1 -> x0, waiting for transfers between devices: 132 us -> none  [local_grads(): b_full = lax.all_gather(act_b, 'dap', axis=1, tiled=True)]
    dot_general x1 -> x0, local copies, waits for them, and re-layouts: 56.6 us -> none  [local_grads(): jnp.einsum('cij,cik->cjk', d_tri, act_a, preferred_element_type=jnp.float32)]
    convert_element_type x11 -> x0, other arithmetic: 34.7 us -> none  [the longest x1 17 us: input_side(): act_a = (mask_f * sig_a * proj_a).astype(jnp.bfloat16)]
    reduce_sum x6 -> x9, other arithmetic: 39.2 us -> 6.83 us  [the longest x5 4.2 us: local_grads(): tail = lambda acc: acc.sum((-2, -1))]
    mul x1 -> x0, other arithmetic: 27.1 us -> none  [input_backward(): grad_a * sig_a]
  transfers between devices with their start and end apart: 2 -> 0, of which waited for: 2 -> 0; matrix products, arithmetic and copies ran while one was open for 10% -> 0% of each run, Pallas kernels for 0% -> 0%
where the time goes in v2:
time: 311 us; the launch traced here: 310 us
  Pallas kernels  264 us (85%)
  blocking collectives  28.5 us (9%)
  local copies, waits for them, and re-layouts  8.78 us (3%)
  other arithmetic  7.11 us (2%)
    pallas_call x1, Pallas kernels, local_grads(): pl.pallas_call(functools.partial(front_kernel, n_dap), name='front', out_...  223 us
    pallas_call x1, Pallas kernels, call(): pl.pallas_call(kernel, name=name, cost_estimate=cost, compiler_params=plt...  41.4 us
    psum x1, blocking collectives, local_grads(): summed = [piece.astype(BF16) for piece in lax.psum(partial, 'dap')]  28.5 us

profile of v2, /device:TPU:112, one launch (start us, length us, event | category | flops | bytes accessed | tf_op | source)
XLA Modules:
  0.0 309.6 jit_solution(2346745448822263163)
XLA Ops:
  0.6 4.7 %concatenate.44 = bf16[640]{0:T(1024)(128)(2,1)S(1)} concatenate(bf16[64]{0:T(256)(128)(2,1)} %param.16, bf16[64]{0:T(256)(128)(2,1)} %param.17, bf16[64]{0:T(256)(128)(2,1)} %param.20, bf16[64]{0:T(256)(128)(2,1)} %param.21, bf16[64]{0:T(256)(128)(2,1)} %param.23, bf16[64]{0:T(256)(128)(2,1)} %param.25, bf16[256]{0:T(256)(128)(2,1)} %param.19), dimensions={0} | concatenate | bytes 2560 | tf_op jit(solution)/shard_map/concatenate | solution.py:484
  5.4 0.7 reshape.31.vecs
  6.1 223.0 %front.1 = (bf16[64,64,512]{2,1,0:T(8,128)(2,1)}, bf16[32,64,512]{2,1,0:T(8,128)(2,1)}, bf16[32,64,512]{2,1,0:T(8,128)(2,1)}, bf16[64,64,512]{2,1,0:T(8,128)(2,1...) custom-call(bf16[1,64,64,512]{3,2,1,0:T(8,128)(2,1)} %bitcast.21, ...), custom_call_target="tpu_custom_call" | custom-call | flops 99999997952 | bytes 1048576 | tf_op jit(solution)/shard_map/front/pallas_call | solution.py:495
  229.1 0.0 copy-start.4
  229.1 41.4 %input_side.1 = (bf16[64,64,512]{2,1,0:T(8,128)(2,1)}, f32[64,2560]{1,0:T(8,128)}, f32[256,8,128]{2,1,0:T(8,128)}, f32[64,512]{1,0:T(8,128)}, f32[64,512]{1,0:T(8,128)}) custom-call(bf16[64,64,512]{2,1,0:T(8,128)(2,1)} %bitcast.22, bf16[64,64,512]{2,1,0:T(8,128)(2,1)} %bitcast.24, s32[64,512]{1,0:T(8,128)} %mask_ref.1, ...), custom_call_target="tpu_custom_call" | custom-call | flops 20999999488 | bytes 1048576 | tf_op jit(solution)/shard_map/input_side/pallas_call | solution.py:463
  270.5 0.0 copy-start
  270.5 0.0 copy-start.3
  270.5 0.0 copy-start.2
  270.5 0.0 copy-start.1
  270.5 1.1 reduce_sum.81
  271.7 1.0 reduce_sum.82
  272.7 1.5 copy.32
  274.2 0.4 bitcast_reduce_fusion
  274.6 0.0 copy-done.4
  274.7 0.1 copy.33
  274.8 0.1 bitcast_reduce_fusion.1
  274.9 0.1 copy.36
  275.0 0.0 copy-done
  275.0 1.0 reduce_sum.84
  276.0 0.1 fusion.3
  276.1 0.1 broadcast_select_fusion.5
  276.2 0.1 pad_maximum_fusion.1
  276.3 1.5 reduce_sum.86
  277.8 0.1 fusion.4
  277.9 0.0 copy-done.3
  277.9 0.6 reduce_sum.85
  278.4 0.1 fusion.5
  278.5 0.1 broadcast_select_fusion
  278.6 0.0 copy-done.2
  278.6 0.6 reduce_sum.88
  279.1 0.0 copy-done.1
  279.1 0.6 reduce_sum.89
  279.7 28.5 %all-reduce = (bf16[64]{0:T(256)(128)(2,1)}, bf16[64]{0:T(256)(128)(2,1)}, bf16[256,64]{1,0:T(8,128)(2,1)S(1)}, bf16[256]{0:T(256)(128)(2,1)}, bf16[64]{0:T(256)...) all-reduce(f32[64]{0:T(128)S(1)} %reduce_sum.81, ...), channel_id=1, replica_groups=mesh['batch'=2,'dap'=8] {'dap'}, use_global_device_ids=true, to_apply=%region_1.2 | all-reduce | flops 25216 | bytes 151296 | tf_op jit(solution)/shard_map/psum | solution.py:527
  308.2 0.7 copy.37
  308.9 0.7 copy.38
  (4 shorter events, 0.1 us)
Async XLA Ops:
  229.1 45.6 %copy-start.4 = (f32[64,512]{1,0:T(8,128)S(1)}, f32[64,512]{1,0:T(8,128)}, u32[]{:S(2)}) copy-start(f32[64,512]{1,0:T(8,128)} %get-tuple-element.46) | copy-start | bytes 393220
  270.5 4.5 %copy-start = (f32[256,8,128]{2,1,0:T(8,128)S(1)}, f32[256,8,128]{2,1,0:T(8,128)}, u32[]{:S(2)}) copy-start(f32[256,8,128]{2,1,0:T(8,128)} %get-tuple-element.43) | copy-start | bytes 3145732
  270.5 7.4 %copy-start.3 = (f32[64,8,128]{2,1,0:T(8,128)S(1)}, f32[64,8,128]{2,1,0:T(8,128)}, u32[]{:S(2)}) copy-start(f32[64,8,128]{2,1,0:T(8,128)} %get-tuple-element.44) | copy-start | bytes 786436
  270.5 8.1 %copy-start.2 = (f32[64,8,128]{2,1,0:T(8,128)S(1)}, f32[64,8,128]{2,1,0:T(8,128)}, u32[]{:S(2)}) copy-start(f32[64,8,128]{2,1,0:T(8,128)} %get-tuple-element.47) | copy-start | bytes 786436
  270.5 8.6 %copy-start.1 = (f32[64,8,128]{2,1,0:T(8,128)S(1)}, f32[64,8,128]{2,1,0:T(8,128)}, u32[]{:S(2)}) copy-start(f32[64,8,128]{2,1,0:T(8,128)} %get-tuple-element.48) | copy-start | bytes 786436

commit v3 on v2

v3 whole, which is shorter than its diff:
```python
import functools
import jax
import jax.numpy as jnp
from jax import lax
from jax.experimental import pallas as pl
from jax.experimental.pallas import tpu as pltpu
from jax.sharding import PartitionSpec as P

LN_EPS = 1e-5
F32 = jnp.float32
BF16 = jnp.bfloat16
SUB = 8
VMEM_LIMIT = 63 * 1024 * 1024
COST = 5e8
ZERO, ONE, TWO = range(3)
LANES = 128


def nn_dot(lhs, rhs):
    return lax.dot_general(lhs, rhs, (((ONE,), (ZERO,)), ((), ())), preferred_element_type=F32)


def nt_dot(lhs, rhs):
    return lax.dot_general(lhs, rhs, (((ONE,), (ONE,)), ((), ())), preferred_element_type=F32)


def tn_dot(lhs, rhs):
    return lax.dot_general(lhs, rhs, (((ZERO,), (ZERO,)), ((), ())), preferred_element_type=F32)


def row_norm(z8, scale, offset):
    mean_val = jnp.mean(z8, axis=ONE, keepdims=True)
    centered = z8 - mean_val
    inv_std = lax.rsqrt(jnp.mean(centered * centered, axis=ONE, keepdims=True) + LN_EPS)
    z_hat = centered * inv_std
    return z_hat, inv_std, (z_hat * scale[None] + offset[None]).astype(BF16)


def lanes(bias, width):
    return jnp.concatenate([bias] * (width // bias.shape[-ONE]), axis=-ONE)


def gated(prod, bias_ref, start, chans, mask_half):
    cols = prod.shape[-ONE]
    val = prod[:chans * SUB].reshape(chans, SUB, cols) + lanes(bias_ref[start:start + chans], cols)
    gate = prod[chans * SUB:].reshape(chans, SUB, cols) + lanes(bias_ref[start + chans:start + TWO * chans], cols)
    return (jnp.tanh(gate) + 1.0) * (val * mask_half[None])


def build_weights(core, w_in, w_out, w_gate, vecs, wk_ref, wg_ref, bias_ref, sc_ref, off_ref, perm_s, wok_s, wotk_s, bo_s, osc_s, ooff_s):
    cz = w_in.shape[ZERO]
    ch = w_in.shape[ONE] // 4
    big = ch * SUB

    def iota(shape, dim):
        return lax.broadcasted_iota(jnp.int32, shape, dim)

    def one(cond):
        return jnp.where(cond, 1.0, 0.0).astype(BF16)

    turn = core * (ch // TWO)
    rep = iota((big, ch), ZERO) // SUB == iota((big, ch), ONE)
    rep_c = lax.rem(iota((big, ch), ZERO) // SUB + turn, ch) == iota((big, ch), ONE)
    rep_t = iota((ch, big), ONE) // SUB == iota((ch, big), ZERO)
    rep_ct = lax.rem(iota((ch, big), ONE) // SUB + turn, ch) == iota((ch, big), ZERO)
    tile = one(iota((cz, SUB * cz), ONE) % cz == iota((cz, SUB * cz), ZERO))
    tile_t = one(iota((SUB * cz, cz), ZERO) % cz == iota((SUB * cz, cz), ONE))
    keep = iota((big, SUB * cz), ZERO) % SUB == iota((big, SUB * cz), ONE) // cz
    keep_t = iota((SUB * cz, big), ONE) % SUB == iota((SUB * cz, big), ZERO) // cz
    same = iota((big, big), ZERO) % SUB == iota((big, big), ONE) % SUB

    def spread(wide):
        return jnp.where(keep, nn_dot(wide, tile), 0.0).astype(BF16)

    def column(sel, row, width):
        picked = jnp.where(sel, jnp.broadcast_to(row.astype(F32), sel.shape), 0.0).astype(BF16)
        return nn_dot(picked, jnp.ones((sel.shape[ONE], width), BF16))

    def eights(sel, row):
        return column(sel, row, LANES).reshape(ch, SUB, LANES)

    for dst, src, scale in ((ZERO, ZERO, 1.0), (ONE, TWO, 0.5), (TWO, ONE, 1.0), (3, 3, 0.5), (4, None, 1.0)):
        w_part = w_gate[...] if src is None else w_in[:, src * ch:(src + ONE) * ch]
        sel, sel_t = (rep, rep_t) if src is None else (rep_c, rep_ct)
        at = slice(dst * big, (dst + ONE) * big)
        wide = (nt_dot(one(sel), w_part) * scale).astype(BF16)
        wk_ref[at] = spread(wide)
        wg_ref[:, at] = jnp.where(keep_t, nn_dot(tile_t, nn_dot(w_part, one(sel_t)).astype(BF16)), 0.0).astype(BF16)
        vec = 5 if src is None else 6 + src
        bias_ref[dst * ch:(dst + ONE) * ch] = eights(sel, vecs[vec]) * scale
    eye = iota((cz, cz), ZERO) == iota((cz, cz), ONE)
    perm_s[...] = spread(one(rep))
    wok_s[...] = jnp.where(same, nn_dot(nt_dot(one(rep), w_out[...]).astype(BF16), one(rep_ct)), 0.0).astype(BF16)
    wotk_s[...] = jnp.where(same, nn_dot(nn_dot(one(rep_c), w_out[...]).astype(BF16), one(rep_t)), 0.0).astype(BF16)
    sc_ref[...] = column(eye, vecs[ZERO], sc_ref.shape[ONE])
    off_ref[...] = column(eye, vecs[ONE], off_ref.shape[ONE])
    osc_s[...] = eights(rep_c, vecs[TWO])
    ooff_s[...] = eights(rep_c, vecs[3])
    bo_s[...] = eights(rep, vecs[4])


def gate_parts(prod, bias_ref, start, chans):
    cols = prod.shape[-ONE]
    val = prod[:chans * SUB].reshape(chans, SUB, cols) + lanes(bias_ref[start:start + chans], cols)
    gate = prod[chans * SUB:].reshape(chans, SUB, cols) + lanes(bias_ref[start + chans:start + TWO * chans], cols)
    return val, jnp.tanh(gate) * 0.5 + 0.5


def project(z8, mask_half, wk_ref, bias_ref, sc_ref, off_ref, chans):
    cols = z8.shape[-ONE]
    _, _, zn = row_norm(z8.astype(F32), sc_ref[...], off_ref[...])
    zn2 = zn.reshape(SUB * zn.shape[ONE], cols)
    n_p = TWO * chans * SUB
    act_a = gated(nn_dot(wk_ref[:n_p], zn2), bias_ref, ZERO, chans, mask_half)
    act_b = gated(nn_dot(wk_ref[n_p:TWO * n_p], zn2), bias_ref, TWO * chans, chans, mask_half)
    return act_a, act_b, zn2


MESH = pl.DeviceIdType.MESH
OWN, LEFT, RIGHT, OPP = range(4)
HOPS = (ZERO, -ONE, ONE, TWO)


def blk(shape, index_map):
    return pl.BlockSpec(shape, index_map)


def front_kernel(n_dap, z_own, dy_ref, m_own, w_in, w_out, w_gate, v_is, v_io, v_os, v_oo, v_bo, v_bg, v_bi,
                 da_ref, keep_ref, got_ref, dgl_ref, gram_ref, dbg_ref, dbo_ref, dsc_ref, dof_ref, wg_ref, sc_ref, off_ref,
                 sv_ref, give_ref, z_far, m_far, a_all, b_pair, a_sib, lg_ref, dyt_ref, do_out, do_in,
                 wk_ref, bias_ref, perm_ref, wo_ref, wot_ref, bout_ref, osc_ref, ooff_ref,
                 o_s, gram_s, lg_v, dyt_v, do_v, dgl_v, send_sem, recv_sem, loc_sem):
    n_chip = n_dap // TWO
    _, rows, cz, cols = z_own.shape
    z_ref, mask_ref = z_own.at[ZERO], m_own.at[ZERO]
    chans = a_all.shape[ONE]
    half = chans // TWO
    hr = rows // TWO
    jb = TWO * rows
    grp = TWO * SUB
    me = lax.axis_index('dap')
    core, chip = lax.rem(me, TWO), me // TWO
    low = core == ZERO

    def peer(hop, flip):
        to = lax.rem(chip + (hop + n_chip), n_chip) * TWO
        return {'dap': to + (ONE - core if flip else core)}

    def copy(k, src, dst, hop, flip):
        return pltpu.make_async_remote_copy(src_ref=src, dst_ref=dst, send_sem=send_sem.at[k], recv_sem=recv_sem.at[k],
                                            device_id=peer(hop, flip), device_id_type=MESH)

    barrier = pltpu.get_barrier_semaphore()
    for hop in HOPS:
        for flip in (ZERO, ONE):
            if hop or flip:
                pl.semaphore_signal(barrier, inc=ONE, device_id=peer(hop, flip), device_id_type=MESH)
    pl.semaphore_wait(barrier, n_dap - ONE)

    n_grp = rows // grp
    masks = [copy(i, mask_ref, m_far.at[i], hop, ZERO) for i, hop in enumerate((ONE, -ONE, TWO))]
    quarter = lambda q: pl.ds(pl.multiple_of(q * grp, grp), grp)
    z_r = lambda q: copy(3 + q, z_ref.at[quarter(q)], z_far.at[ZERO, quarter(q)], ONE, ZERO)
    z_l = lambda q: copy(3 + n_grp + q, z_ref.at[quarter(q)], z_far.at[ONE, quarter(q)], -ONE, ZERO)
    fwd_r = lambda q: copy(3 + TWO * n_grp + q, z_far.at[ZERO, quarter(q)], z_far.at[TWO, quarter(q)], ONE, ZERO)
    fwd_l = lambda q: copy(3 + TWO * n_grp + q, z_far.at[ONE, quarter(q)], z_far.at[TWO, quarter(q)], -ONE, ZERO)
    base_b = 3 + 3 * n_grp
    my_rows = pl.multiple_of(core * rows, rows)

    def swap_b(r, q):
        at = pl.ds(pl.multiple_of(my_rows + q * grp, grp), grp)
        return [copy(base_b + (r * n_grp + q) * TWO + h, b_pair.at[r, pl.ds(h * half, half), at], b_pair.at[r, pl.ds((ONE - h) * half, half), at], ZERO, ONE) for h in (ZERO, ONE)]

    base_a = base_b + 8 * n_grp
    swap_a = lambda r, q: copy(base_a + r * n_grp + q, a_all.at[r, pl.ds(half, half), quarter(q)], a_sib.at[r, :, quarter(q)], ZERO, ONE)
    base_s = base_a + 4 * n_grp
    back = (OWN, RIGHT, LEFT, OPP)
    ship = [[None if (r == OWN and side == ZERO) else
             copy(base_s + TWO * r + side, do_out.at[r, pl.ds(side * half, half)], do_in.at[back[r], side], HOPS[r], side) for side in (ZERO, ONE)] for r in range(4)]
    swap_d = [copy(base_s + 8 + q, give_ref.at[pl.ds(q * (half // TWO), half // TWO)], got_ref.at[pl.ds(q * (half // TWO), half // TWO)], ZERO, ONE) for q in (ZERO, ONE)]

    for c in masks:
        c.start()
    for q in range(n_grp):
        z_r(q).start()
        z_l(n_grp - ONE - q).start()
    b_all = v_bi[...]
    vecs = [ref[...] for ref in (v_is, v_io, v_os, v_oo, v_bo, v_bg)] + [b_all[:, i * chans:(i + ONE) * chans] for i in range(4)]
    build_weights(core, w_in, w_out, w_gate, vecs, wk_ref, wg_ref, bias_ref, sc_ref, off_ref, perm_ref, wo_ref, wot_ref, bout_ref, osc_ref, ooff_ref)

    row3 = blk((grp, cz, cols), lambda g: (g, ZERO, ZERO))
    row2 = blk((grp, cols), lambda g: (g, ZERO))
    chan3 = lambda n: blk((n, grp, cols), lambda g: (ZERO, g, ZERO))

    def ab_body(z_b, m_b, a_b, b_b):
        a_parts, b_parts = [], []
        for h in range(TWO):
            rws = slice(h * SUB, (h + ONE) * SUB)
            act_a, act_b, _ = project(z_b[ZERO, rws], m_b[ZERO, rws].astype(F32) * 0.5, wk_ref, bias_ref, sc_ref, off_ref, chans)
            a_parts.append(act_a)
            b_parts.append(act_b)
        a_b[ZERO] = jnp.concatenate(a_parts, axis=ONE).astype(BF16)
        b_b[ZERO] = jnp.concatenate(b_parts, axis=ONE).astype(BF16)

    def own_body(z_b, m_b, a_b, b_b, sv_b):
        acts = ([], [])
        for h in range(TWO):
            rws = slice(h * SUB, (h + ONE) * SUB)
            _, _, zn = row_norm(z_b[ZERO, rws].astype(F32), sc_ref[...], off_ref[...])
            zn2 = zn.reshape(SUB * cz, cols)
            mask = m_b[ZERO, rws].astype(F32)[None]
            n_p = TWO * chans * SUB
            for side in (ZERO, ONE):
                val, sig = gate_parts(nn_dot(wk_ref[side * n_p:(side + ONE) * n_p], zn2), bias_ref, TWO * side * chans, chans)
                sv_b[TWO * side, :, rws] = val
                sv_b[TWO * side + ONE, :, rws] = sig
                acts[side].append(mask * sig * val)
        a_b[ZERO] = jnp.concatenate(acts[ZERO], axis=ONE).astype(BF16)
        b_b[ZERO] = jnp.concatenate(acts[ONE], axis=ONE).astype(BF16)

    def project_rows(z_src, m_src, n, slot, place):
        pltpu.emit_pipeline(
            ab_body, grid=(n,),
            in_specs=[blk((ONE, grp, cz, cols), lambda g: (slot(g), place(g)[ONE], ZERO, ZERO)), blk((ONE, grp, cols), lambda g: (slot(g), place(g)[ONE], ZERO))],
            out_specs=[blk((ONE, chans, grp, cols), lambda g: (place(g)[ZERO], ZERO, place(g)[ONE], ZERO)),
                       blk((ONE, chans, grp, cols), lambda g: (place(g)[ZERO], ZERO, core * n_grp + place(g)[ONE], ZERO))])(z_src, m_src, a_all, b_pair)

    def swap(r, q):
        for c in swap_b(r, q):
            c.start()
        swap_a(r, q).start()

    def swapped_b(r):
        def body(q, carry):
            for c in swap_b(r, q):
                c.wait_recv()
            return carry
        lax.fori_loop(ZERO, n_grp, body, ZERO)

    def lg_body(z_b, dy_b, lg_b, dyt_b):
        dy_parts = []
        for h in range(TWO):
            rws = slice(h * SUB, (h + ONE) * SUB)
            _, _, zn = row_norm(z_b[rws].astype(F32), sc_ref[...], off_ref[...])
            zn2 = zn.reshape(SUB * cz, cols)
            lg_b[:, rws, :] = nn_dot(wk_ref[4 * chans * SUB:], zn2).reshape(cz, SUB, cols) + lanes(bias_ref[4 * chans:], cols)
            dy_parts.append(nn_dot(perm_ref[...], dy_b[rws].reshape(SUB * cz, cols)).reshape(cz, SUB, cols))
        dyt_b[...] = jnp.concatenate(dy_parts, axis=ONE).astype(BF16)

    for ref in (dbg_ref, dbo_ref, dsc_ref, dof_ref, gram_s):
        ref[...] = jnp.zeros_like(ref)

    per = chans // 8

    def o_body(a_b, b_b):
        base = pl.program_id(ZERO) * per
        for c in range(per):
            o_s[base + c] = nt_dot(a_b[c], b_b[c])

    def chain(r):
        where = lax.rem(chip + (HOPS[r] + n_chip), n_chip)
        col = pl.ds(pl.multiple_of(where * jb, jb), jb)
        get_lg = pltpu.make_async_copy(lg_ref.at[:, :, col], lg_v, loc_sem.at[ZERO])
        get_dy = pltpu.make_async_copy(dyt_ref.at[:, :, col], dyt_v, loc_sem.at[ONE])
        get_lg.start()
        get_dy.start()
        pltpu.emit_pipeline(o_body, grid=(8,), in_specs=[blk((per, rows, cols), lambda s: (s, ZERO, ZERO)), blk((per, jb, cols), lambda s: (s, ZERO, ZERO))])(
            a_all.at[OWN], b_pair.at[r])
        get_lg.wait()
        get_dy.wait()

        def chain_body(g, carry):
            pair = pl.ds(pl.multiple_of(g * TWO * SUB, TWO * SUB), TWO * SUB)

            def wide(ref):
                val = ref[:, pair, :].astype(F32)
                return jnp.concatenate([val[:, :SUB], val[:, SUB:]], axis=TWO)

            def tall(val):
                return jnp.concatenate([val[..., :jb], val[..., jb:]], axis=ONE)

            def add(ref, val):
                ref[...] += val[..., :jb] + val[..., jb:]

            twice = lambda ref: lanes(ref[...], TWO * jb)
            o8 = wide(o_s)
            centered = o8 - jnp.mean(o8, axis=ZERO, keepdims=True)
            inv_std = lax.rsqrt(jnp.mean(centered * centered, axis=ZERO, keepdims=True) + LN_EPS)
            o_hat = centered * inv_std
            o_norm = (o_hat * twice(osc_ref) + twice(ooff_ref)).astype(BF16).reshape(chans * SUB, TWO * jb)
            upd = (nn_dot(wo_ref[...], o_norm).reshape(cz, SUB, TWO * jb) + twice(bout_ref)).astype(BF16).astype(F32)
            sig = jnp.tanh(wide(lg_v) * 0.5) * 0.5 + 0.5
            prod = sig * wide(dyt_v)
            d_upd = prod.astype(BF16)
            dgl = prod * upd * (1.0 - sig)
            add(dbg_ref, dgl)
            dgl_v[:, pair, :] = tall(dgl).astype(BF16)
            add(dbo_ref, d_upd.astype(F32))
            d_upd2 = d_upd.reshape(cz * SUB, TWO * jb)
            gram_s[...] += nt_dot(o_norm, d_upd2)
            d_on = nn_dot(wot_ref[...], d_upd2).astype(BF16).astype(F32).reshape(chans, SUB, TWO * jb)
            add(dsc_ref, d_on * o_hat)
            add(dof_ref, d_on)
            g_hat = d_on * twice(osc_ref)
            m1 = jnp.mean(g_hat, axis=ZERO, keepdims=True)
            m2 = jnp.mean(g_hat * o_hat, axis=ZERO, keepdims=True)
            do_v[:, pair, :] = tall(inv_std * (g_hat - m1 - o_hat * m2)).astype(BF16)
            return carry
        lax.fori_loop(ZERO, rows // (TWO * SUB), chain_body, ZERO)
        put_do = pltpu.make_async_copy(do_v, do_out.at[r], loc_sem.at[ZERO])
        put_gl = pltpu.make_async_copy(dgl_v, dgl_ref.at[:, :, col], loc_sem.at[ONE])
        put_do.start()
        put_gl.start()
        put_do.wait()
        put_gl.wait()
        for c in ship[r]:
            if c is not None:
                c.start()

    pltpu.emit_pipeline(
        own_body, grid=(n_grp,),
        in_specs=[blk((ONE, grp, cz, cols), lambda g: (ZERO, g, ZERO, ZERO)), blk((ONE, grp, cols), lambda g: (ZERO, g, ZERO))],
        out_specs=[blk((ONE, chans, grp, cols), lambda g: (OWN, ZERO, g, ZERO)), blk((ONE, chans, grp, cols), lambda g: (OWN, ZERO, core * n_grp + g, ZERO)),
                   blk((4, chans, grp, cols), lambda g: (ZERO, ZERO, g, ZERO))])(z_own, m_own, a_all, b_pair, sv_ref)
    for q in range(n_grp):
        swap(OWN, q)
    pltpu.emit_pipeline(lg_body, grid=(n_grp,), in_specs=[row3, row3], out_specs=[chan3(cz), chan3(cz)])(z_own.at[ZERO], dy_ref, lg_ref, dyt_ref)
    swapped_b(OWN)
    chain(OWN)
    for c in masks:
        c.wait_recv()

    def sides(t, carry):
        z_r(t).wait_recv()
        z_l(n_grp - ONE - t).wait_recv()

        @pl.when(t < n_grp // TWO)
        def _():
            fwd_r(t).start()
            fwd_l(n_grp - ONE - t).start()
        project_rows(z_far, m_far, TWO, lambda g: g, lambda g: (g + LEFT, jnp.where(g == ZERO, t, n_grp - ONE - t)))
        swap(LEFT, t)
        swap(RIGHT, n_grp - ONE - t)
        return carry
    lax.fori_loop(ZERO, n_grp, sides, ZERO)
    swapped_b(LEFT)
    chain(LEFT)
    swapped_b(RIGHT)
    chain(RIGHT)

    def opposite(t, carry):
        fwd_r(t).wait_recv()
        fwd_l(n_grp - ONE - t).wait_recv()
        project_rows(z_far, m_far, TWO, lambda g: TWO, lambda g: (OPP, jnp.where(g == ZERO, t, n_grp - ONE - t)))
        swap(OPP, t)
        swap(OPP, n_grp - ONE - t)
        return carry
    lax.fori_loop(ZERO, n_grp // TWO, opposite, ZERO)
    swapped_b(OPP)
    chain(OPP)

    gram = gram_s[...]
    n = gram.shape[ZERO]
    diag = lax.broadcasted_iota(jnp.int32, (n, n), ZERO) % SUB == lax.broadcasted_iota(jnp.int32, (n, n), ONE) % SUB
    gram_ref[...] = jnp.sum(jnp.where(diag, gram, 0.0).reshape(chans, SUB, n), axis=ONE)

    pc = 4
    n_a = chans // pc

    def da_body(do_b, b_b, da_b):
        for c in range(pc):
            lhs = jnp.concatenate([do_b[r, c] for r in range(4)], axis=ONE)
            rhs = jnp.concatenate([b_b[r, c] for r in range(4)], axis=ZERO)
            da_b[c] = nn_dot(lhs, rhs).astype(BF16)

    pltpu.emit_pipeline(
        da_body, grid=(n_a,),
        in_specs=[blk((4, pc, rows, jb), lambda s: (ZERO, s, ZERO, ZERO)), blk((4, pc, jb, cols), lambda s: (ZERO, s, ZERO, ZERO))],
        out_specs=[blk((pc, rows, cols), lambda s: (s, ZERO, ZERO))])(do_out, b_pair, da_ref)

    for r in range(4):
        lax.fori_loop(ZERO, n_grp, lambda q, carry, r=r: (swap_a(r, q).wait_recv(), carry)[ONE], ZERO)
        for c in ship[r]:
            if c is not None:
                c.wait_recv()

    def db_body(own_b, do0_b, do1_b, am_b, as_b, keep_b, give_b):
        for c in range(pc):
            lhs, rhs = [], []
            for r in range(4):
                lhs += [own_b[ZERO, c] if r == OWN else do0_b[r - ONE, c], do1_b[r, ZERO, c]]
                rhs += [am_b[r, c], as_b[r, c]]
            pair = tn_dot(jnp.concatenate(lhs, axis=ZERO), jnp.concatenate(rhs, axis=ZERO)).astype(BF16)
            keep_b[c] = jnp.where(low, pair[:rows], pair[rows:])
            give_b[c] = jnp.where(low, pair[rows:], pair[:rows])

    for q in (ZERO, ONE):
        steps = half // pc // TWO
        at = lambda s: s + q * steps
        c3 = blk((pc, rows, cols), lambda s: (at(s), ZERO, ZERO))
        pltpu.emit_pipeline(
            db_body, grid=(steps,),
            in_specs=[blk((ONE, pc, rows, jb), lambda s: (ZERO, at(s), ZERO, ZERO)), blk((3, pc, rows, jb), lambda s: (ZERO, at(s), ZERO, ZERO)),
                      blk((4, ONE, pc, rows, jb), lambda s: (ZERO, ZERO, at(s), ZERO, ZERO)),
                      c4_at(pc, rows, cols, at), c4_at(pc, rows, cols, at)],
            out_specs=[c3, c3])(do_out, do_in.at[pl.ds(ONE, 3), ZERO], do_in.at[:, pl.ds(ONE, ONE)], a_all, a_sib, keep_ref, give_ref)
        swap_d[q].start()
    for c in swap_d:
        c.wait_recv()
    for c in masks + swap_d + [c for pair in ship for c in pair if c is not None]:
        c.wait_send()

    def sent(q, carry):
        z_r(q).wait_send()
        z_l(q).wait_send()
        for r in range(4):
            for c in swap_b(r, q) + [swap_a(r, q)]:
                c.wait_send()

        @pl.when(q < n_grp // TWO)
        def _():
            fwd_r(q).wait_send()

        @pl.when(q >= n_grp // TWO)
        def _():
            fwd_l(q).wait_send()
        return carry
    lax.fori_loop(ZERO, n_grp, sent, ZERO)


def c4_at(pc, rows, cols, at):
    return pl.BlockSpec((4, pc, rows, cols), lambda s: (ZERO, at(s), ZERO, ZERO))


def input_kernel(z_ref, dy_ref, mask_ref, da_ref, db0_ref, db1_ref, dgl_ref, sv_ref, wg_ref, sc_ref, off_ref,
                 dz_ref, gram_ref, dbias_ref, dsc_ref, dof_ref, dp_s):
    chans = da_ref.shape[ZERO]
    chan_z, cols = z_ref.shape[ONE:]

    @pl.when(pl.program_id(ZERO) == ZERO)
    def _():
        for ref in (gram_ref, dbias_ref, dsc_ref, dof_ref):
            ref[...] = jnp.zeros_like(ref)

    def fold(val):
        acc = val[..., :LANES]
        for lane in range(LANES, cols, LANES):
            acc = acc + val[..., lane:lane + LANES]
        return acc

    n_p = chans * SUB
    grads = (da_ref[...].astype(F32), jnp.concatenate([db0_ref[...], db1_ref[...]], axis=ZERO).astype(F32))
    for half in range(TWO):
        rows = slice(half * SUB, (half + ONE) * SUB)
        z_hat, inv_std, zn = row_norm(z_ref[rows].astype(F32), sc_ref[...], off_ref[...])
        zn2 = zn.reshape(SUB * chan_z, cols)
        mask_f = mask_ref[rows].astype(F32)[None]
        for side, grad_all in enumerate(grads):
            val, sig = sv_ref[TWO * side, :, rows], sv_ref[TWO * side + ONE, :, rows]
            grad = grad_all[:, rows] * mask_f
            d_val = grad * sig
            d_gate = d_val * val * (1.0 - sig)
            dbias_ref[TWO * side * chans:(TWO * side + ONE) * chans] += fold(d_val)
            dbias_ref[(TWO * side + ONE) * chans:(TWO * side + TWO) * chans] += fold(d_gate)
            dp_s[TWO * side * n_p:(TWO * side + ONE) * n_p] = d_val.astype(BF16).reshape(n_p, cols)
            dp_s[(TWO * side + ONE) * n_p:(TWO * side + TWO) * n_p] = d_gate.astype(BF16).reshape(n_p, cols)
        dp_s[4 * n_p:] = dgl_ref[...].astype(F32)[:, rows].astype(BF16).reshape(n_p, cols)
        d_zn = nn_dot(wg_ref[...], dp_s[...]).astype(BF16).astype(F32).reshape(SUB, chan_z, cols)
        gram = nt_dot(zn2, dp_s[...]).reshape(SUB, chan_z, dp_s.shape[ZERO])
        lane_row = lax.broadcasted_iota(jnp.int32, (chan_z, dp_s.shape[ZERO]), ONE) % SUB
        acc = gram_ref[...]
        for i in range(SUB):
            acc = acc + jnp.where(lane_row == i, gram[i], 0.0)
        gram_ref[...] = acc
        dsc_ref[...] += jnp.sum(d_zn * z_hat, axis=ZERO)
        dof_ref[...] += jnp.sum(d_zn, axis=ZERO)
        g_hat = d_zn * sc_ref[...][None]
        m1 = jnp.mean(g_hat, axis=ONE, keepdims=True)
        m2 = jnp.mean(g_hat * z_hat, axis=ONE, keepdims=True)
        d_z = dy_ref[rows].astype(F32) + inv_std * (g_hat - m1 - z_hat * m2)
        dz_ref[rows] = d_z.astype(BF16)


def exact_dot(lhs, rhs, dims):
    return lax.dot_general(lhs, rhs, (dims, ((), ())), precision=lax.Precision.HIGHEST, preferred_element_type=F32)


def sum_kernel(n_dap, gram_i, dbias, dsc_i, dof_i, gram_o, dsc_o, dof_o, dbo, dbg, out_ref, part_s, in_s, mine_s, send_sem, recv_sem, send2, recv2):
    me = lax.axis_index('dap')
    core = lax.rem(me, TWO)
    low = core == ZERO
    barrier = pltpu.get_barrier_semaphore()
    to = [lax.rem(me + d, n_dap) for d in range(n_dap)]
    for d in range(ONE, n_dap):
        pl.semaphore_signal(barrier, inc=ONE, device_id={'dap': to[d]}, device_id_type=MESH)
    cz = gram_i.shape[ZERO]
    ch = gram_o.shape[ZERO]
    big = ch * SUB
    turn = core * (ch // TWO)
    row = lax.broadcasted_iota(jnp.int32, (big, ch), ZERO) // SUB
    col = lax.broadcasted_iota(jnp.int32, (big, ch), ONE)
    fold = jnp.where(row == col, 1.0, 0.0)
    fold_c = jnp.where(lax.rem(row + turn, ch) == col, 1.0, 0.0)
    part_s[...] = jnp.zeros_like(part_s)
    for dst, src in ((ZERO, ZERO), (ONE, TWO), (TWO, ONE), (3, 3), (4, 4)):
        val = exact_dot(gram_i[:, dst * big:(dst + ONE) * big], fold if src == 4 else fold_c, ((ONE,), (ZERO,)))
        part_s[(src // TWO) * cz:(src // TWO + ONE) * cz, (src % TWO) * ch:(src % TWO + ONE) * ch] = val
    val = exact_dot(gram_o[...], fold, ((ONE,), (ZERO,)))
    h = ch // TWO
    val = jnp.where(low, val, jnp.concatenate([val[h:], val[:h]], axis=ZERO))
    part_s[TWO * cz:3 * cz, ch:TWO * ch] = val
    eye = lax.broadcasted_iota(jnp.int32, (ch, ch), ZERO)
    lane = lax.broadcasted_iota(jnp.int32, (ch, ch), ONE)
    order = jnp.where(lax.rem(eye + turn, ch) == lane, 1.0, 0.0)

    def line(acc, ordered):
        flat = jnp.sum(acc, axis=ONE) if len(acc.shape) == 3 else acc
        res = exact_dot(jnp.ones((SUB, flat.shape[ONE]), F32), flat, ((ONE,), (ONE,)))
        return exact_dot(res, order, ((ONE,), (ZERO,)))[:ONE] if ordered else res[:ONE]

    base = 3 * cz
    for dst, src in ((ZERO, ZERO), (ONE, TWO), (TWO, ONE), (3, 3)):
        part_s[base + src // TWO:base + src // TWO + ONE, (src % TWO) * ch:(src % TWO + ONE) * ch] = line(dbias[dst * ch:(dst + ONE) * ch], True)
    part_s[base + TWO:base + 3, :ch] = line(dsc_i[...], False)
    part_s[base + TWO:base + 3, ch:TWO * ch] = line(dof_i[...], False)
    part_s[base + 3:base + 4, :ch] = line(dsc_o[...], True)
    part_s[base + 3:base + 4, ch:TWO * ch] = line(dof_o[...], True)
    part_s[base + 4:base + 5, :ch] = line(dbo[...], False)
    part_s[base + 4:base + 5, ch:TWO * ch] = line(dbg[...], False)

    pl.semaphore_wait(barrier, n_dap - ONE)
    n = mine_s.shape[ZERO]

    def scatter(d):
        return pltpu.make_async_remote_copy(src_ref=part_s.at[pl.ds(pl.multiple_of(to[d] * n, n), n)], dst_ref=in_s.at[d - ONE],
                                            send_sem=send_sem.at[d - ONE], recv_sem=recv_sem.at[d - ONE],
                                            device_id={'dap': to[d]}, device_id_type=MESH)

    at = pl.ds(pl.multiple_of(me * n, n), n)

    def spread(d):
        return pltpu.make_async_remote_copy(src_ref=mine_s, dst_ref=out_ref.at[at], send_sem=send2.at[d - ONE], recv_sem=recv2.at[d - ONE],
                                            device_id={'dap': to[d]}, device_id_type=MESH)

    for d in range(ONE, n_dap):
        scatter(d).start()
    total = part_s[at]
    for d in range(ONE, n_dap):
        scatter(d).wait_recv()
        total = total + in_s[d - ONE]
    mine_s[...] = total
    for d in range(ONE, n_dap):
        spread(d).start()
    out_ref[at] = total
    for d in range(ONE, n_dap):
        spread(d).wait_recv()
    for d in range(ONE, n_dap):
        scatter(d).wait_send()
        spread(d).wait_send()


def round_kernel(tot_ref, sc_ref, off_ref, w_ref, b_ref, osc_ref, ooff_ref, wout_ref, bout_ref, wg_ref, bg_ref):
    cz, ch = wg_ref.shape
    tot = tot_ref[...].astype(BF16)
    base = 3 * cz
    w_ref[:, :TWO * ch] = tot[:cz]
    w_ref[:, TWO * ch:] = tot[cz:TWO * cz]
    wg_ref[...] = tot[TWO * cz:3 * cz, :ch]
    wout_ref[...] = tot[TWO * cz:3 * cz, ch:]
    vec = tot_ref[base:base + SUB]
    for ref, r, c in ((b_ref, ZERO, ZERO), (sc_ref, TWO, ZERO), (off_ref, TWO, ONE), (osc_ref, 3, ZERO), (ooff_ref, 3, ONE), (bout_ref, 4, ZERO), (bg_ref, 4, ONE)):
        if ref is b_ref:
            ref[:, :TWO * ch] = vec[ZERO:ONE].astype(BF16)
            ref[:, TWO * ch:] = vec[ONE:TWO].astype(BF16)
        else:
            ref[...] = vec[r:r + ONE, c * ch:(c + ONE) * ch].astype(BF16)


def whole(arr):
    nd = arr.ndim
    return pl.BlockSpec(arr.shape, lambda *_: (ZERO,) * nd, pipeline_mode=pl.Buffered(ONE))


def call(kernel, name, us, *args, **kw):
    cost = pl.CostEstimate(flops=int(us * COST), bytes_accessed=TWO**20, transcendentals=ZERO)
    return pl.pallas_call(kernel, name=name, cost_estimate=cost, compiler_params=pltpu.CompilerParams(vmem_limit_bytes=VMEM_LIMIT), **kw)(*args)


def local_grads(n_dap, z_loc, mask_loc, dy_loc, ln_in_scale, ln_in_offset, w_in, b_in, ln_out_scale, ln_out_offset, w_out, b_out, w_gate, b_gate):
    rows, cols, cz = z_loc.shape
    ch = w_in.shape[ONE] // 4
    half = ch // TWO
    jb = TWO * rows
    grp = TWO * SUB
    n_grp = rows // grp
    sds = jax.ShapeDtypeStruct
    z_t = jnp.transpose(z_loc, (ZERO, TWO, ONE))
    dy_t = jnp.transpose(dy_loc, (ZERO, TWO, ONE))

    n_e = 5 * ch
    b16 = lambda *shape: sds(shape, BF16)
    vecs = [v.reshape(ONE, -ONE) for v in (ln_in_scale, ln_in_offset, ln_out_scale, ln_out_offset, b_out, b_gate, b_in)]
    row3 = lambda nd: pl.BlockSpec((grp, nd, cols), lambda g: (g, ZERO, ZERO))
    chan_rows = lambda n: pl.BlockSpec((n, grp, cols), lambda g: (ZERO, g, ZERO))
    mask_spec = pl.BlockSpec((grp, cols), lambda g: (g, ZERO))
    f32 = lambda *shape: sds(shape, F32)
    any_spec = pl.BlockSpec(memory_space=pl.ANY)
    vmem = pl.BlockSpec(memory_space=pltpu.VMEM)
    n_copy = 3 + 3 * n_grp + 8 * n_grp + 4 * n_grp + 10
    acc = f32(ch, SUB, LANES)
    blocks = pltpu.VMEM((ch * SUB, cz * SUB), BF16)
    spread = pltpu.VMEM((ch, SUB, LANES), F32)
    outs = pl.pallas_call(
        functools.partial(front_kernel, n_dap), name='front',
        out_shape=(b16(ch, rows, cols), b16(half, rows, cols), b16(half, rows, cols), b16(cz, rows, cols), f32(ch, cz * SUB), acc, acc, acc, acc,
                   b16(SUB * cz, n_e * SUB), f32(cz, cols), f32(cz, cols),
                   f32(4, ch, rows, cols), b16(half, rows, cols), b16(3, rows, cz, cols), sds((3, rows, cols), jnp.int32), b16(4, ch, rows, cols), b16(4, ch, jb, cols),
                   b16(4, half, rows, cols), f32(cz, rows, cols), b16(cz, rows, cols), b16(4, ch, rows, jb), b16(4, TWO, half, rows, jb)),
        in_specs=[any_spec] * 3 + [vmem] * 10,
        out_specs=(any_spec,) * 4 + (vmem,) * 8 + (any_spec,) * 11,
        scratch_shapes=[pltpu.VMEM((n_e * SUB, SUB * cz), BF16), pltpu.VMEM((n_e, SUB, LANES), F32), blocks, blocks, blocks, spread, spread, spread,
                        pltpu.VMEM((ch, rows, jb), F32), pltpu.VMEM((ch * SUB, cz * SUB), F32), pltpu.VMEM((cz, rows, jb), F32),
                        pltpu.VMEM((cz, rows, jb), BF16), pltpu.VMEM((ch, rows, jb), BF16), pltpu.VMEM((cz, rows, jb), BF16),
                        pltpu.SemaphoreType.DMA((n_copy,)), pltpu.SemaphoreType.DMA((n_copy,)), pltpu.SemaphoreType.DMA((TWO,))],
        cost_estimate=pl.CostEstimate(flops=10**11, bytes_accessed=TWO**20, transcendentals=ZERO),
        compiler_params=pltpu.CompilerParams(vmem_limit_bytes=VMEM_LIMIT, collective_id=ZERO, has_side_effects=True),
    )(z_t[None], dy_t, mask_loc[None], w_in, w_out, w_gate, *vecs)
    da, keep, got, dgl, gram_o, dbg, dbo, dsc_o, dof_o, wg, sc_in, off_in, sv = outs[:13]

    args = (z_t, dy_t, mask_loc, da, keep, got, dgl, sv, wg, sc_in, off_in)
    const = lambda *shape: pl.BlockSpec(shape, lambda g: (ZERO,) * len(shape))
    dz_t, gram_i, dbias, dsc_i, dof_i = call(
        input_kernel, 'input_side', 42, *args, grid=(n_grp,),
        out_shape=(b16(rows, cz, cols), sds((cz, n_e * SUB), F32), sds((4 * ch, SUB, LANES), F32), sds((cz, cols), F32), sds((cz, cols), F32)),
        in_specs=[row3(cz), row3(cz), mask_spec, chan_rows(ch), chan_rows(half), chan_rows(half), chan_rows(cz),
                  pl.BlockSpec((4, ch, grp, cols), lambda g: (ZERO, ZERO, g, ZERO))] + [whole(x) for x in args[8:]],
        out_specs=(row3(cz), const(cz, n_e * SUB), const(4 * ch, SUB, LANES), const(cz, cols), const(cz, cols)),
        scratch_shapes=[pltpu.VMEM((n_e * SUB, cols), BF16)])

    n_sum = (-(3 * cz + SUB) // (n_dap * SUB)) * -SUB
    total = pl.pallas_call(
        functools.partial(sum_kernel, n_dap), name='weight_sums',
        out_shape=f32(n_sum * n_dap, LANES), in_specs=[vmem] * 9, out_specs=vmem,
        scratch_shapes=[pltpu.VMEM((n_sum * n_dap, LANES), F32), pltpu.VMEM((n_dap - ONE, n_sum, LANES), F32), pltpu.VMEM((n_sum, LANES), F32)]
        + [pltpu.SemaphoreType.DMA((n_dap - ONE,))] * 4,
        cost_estimate=pl.CostEstimate(flops=10**10, bytes_accessed=TWO**20, transcendentals=ZERO),
        compiler_params=pltpu.CompilerParams(vmem_limit_bytes=VMEM_LIMIT, collective_id=ONE, has_side_effects=True),
    )(gram_i, dbias, dsc_i, dof_i, gram_o, dsc_o, dof_o, dbo, dbg)
    row = lambda n: b16(ONE, n)
    grads = call(round_kernel, 'round', ONE, total,
                 out_shape=(row(cz), row(cz), b16(cz, 4 * ch), row(4 * ch), row(ch), row(ch), b16(ch, cz), row(cz), b16(cz, cz), row(cz)))
    grads = [g.reshape(-ONE) if g.shape[ZERO] == ONE else g for g in grads]
    return (jnp.transpose(dz_t, (ZERO, TWO, ONE)), *grads)


def solution(mesh):
    pair_spec = P(('batch', 'dap'), None, None)
    mask_spec = P(('batch', 'dap'), None)
    vec_rep = P(None)
    mat_rep = P(None, None)
    vec_part = P('batch')
    mat_part = P('batch', None)
    in_specs = (pair_spec, mask_spec, pair_spec, vec_rep, vec_rep, mat_rep, vec_rep, vec_rep, vec_rep, mat_rep, vec_rep, mat_rep, vec_rep)
    out_specs = (pair_spec, vec_part, vec_part, mat_part, vec_part, vec_part, vec_part, mat_part, vec_part, mat_part, vec_part)
    body = functools.partial(local_grads, mesh.shape['dap'])
    return jax.shard_map(body, mesh=mesh, in_specs=in_specs, out_specs=out_specs, check_vma=False)
```

time: 311 us -> 279 us (0.90)
  blocking collectives: 28.5 us -> 0 us
  Pallas kernels: 264 us -> 274 us
  local copies, waits for them, and re-layouts: 8.78 us -> 1.22 us
  other arithmetic: 7.11 us -> 1.19 us
    psum x1 -> x0, blocking collectives: 28.5 us -> none  [local_grads(): summed = [piece.astype(BF16) for piece in lax.psum(partial, 'dap')]]
    pallas_call x0 -> x1, Pallas kernels: none -> 13.6 us  [local_grads(): pl.pallas_call(functools.partial(sum_kernel, n_dap), name='weight_sums',...]
    reduce_sum x9 -> x0, other arithmetic: 6.83 us -> none  [the longest x5 4.2 us: local_grads(): tail = lambda acc: acc.sum((-2, -1))]
    concatenate x1 -> x0, local copies, waits for them, and re-layouts: 4.74 us -> none  [local_grads(): jnp.concatenate([ln_in_scale, ln_in_offset, ln_out_scale, ln_out_offset,...]
    pallas_call x1 -> x2, Pallas kernels: 41.4 us -> 38.1 us  [call(): pl.pallas_call(kernel, name=name, cost_estimate=cost, compiler_params=plt...]
where the time goes in v3:
time: 279 us; the launch traced here: 277 us
  Pallas kernels  274 us (98%)
    pallas_call x1, Pallas kernels, local_grads(): pl.pallas_call(functools.partial(front_kernel, n_dap), name='front', out_...  222 us
    pallas_call x2, Pallas kernels, call(): pl.pallas_call(kernel, name=name, cost_estimate=cost, compiler_params=plt...  38.1 us
    pallas_call x1, Pallas kernels, local_grads(): pl.pallas_call(functools.partial(sum_kernel, n_dap), name='weight_sums',...  13.6 us

profile of v3, /device:TPU:112, one launch (start us, length us, event | category | flops | bytes accessed | tf_op | source)
XLA Modules:
  0.0 277.2 jit_solution(10799614458395052455)
XLA Ops:
  0.6 1.2 reshape.70.v_bi
  1.9 222.4 %front.1 = (bf16[64,64,512]{2,1,0:T(8,128)(2,1)}, bf16[32,64,512]{2,1,0:T(8,128)(2,1)}, bf16[32,64,512]{2,1,0:T(8,128)(2,1)}, bf16[64,64,512]{2,1,0:T(8,128)(2,1...) custom-call(bf16[1,64,64,512]{3,2,1,0:T(8,128)(2,1)} %bitcast.18, ...), custom_call_target="tpu_custom_call" | custom-call | flops 99999997952 | bytes 1048576 | tf_op jit(solution)/shard_map/front/pallas_call | solution.py:613
  224.3 36.5 %input_side.1 = (bf16[64,64,512]{2,1,0:T(8,128)(2,1)}, f32[64,2560]{1,0:T(8,128)}, f32[256,8,128]{2,1,0:T(8,128)}, f32[64,512]{1,0:T(8,128)}, f32[64,512]{1,0:T(8,128)}) custom-call(bf16[64,64,512]{2,1,0:T(8,128)(2,1)} %bitcast.19, bf16[64,64,512]{2,1,0:T(8,128)(2,1)} %bitcast.21, s32[64,512]{1,0:T(8,128)} %mask_ref.1, ...), custom_call_target="tpu_custom_call" | custom-call | flops 20999999488 | bytes 1048576 | tf_op jit(solution)/shard_map/input_side/pallas_call | solution.py:586
  260.8 13.6 %weight_sums.1.tot_ref = f32[256,128]{1,0:T(8,128)} custom-call(f32[64,2560]{1,0:T(8,128)} %get-tuple-element.48.gram_i, f32[256,8,128]{2,1,0:T(8,128)} %get-tuple-element.49.dbias, f32[64,512]{1,0:T(8,128)} %get-tuple-element.50.dsc_i, f32[64,512]{1,0:T(8,128)} %get-tuple-element.51.dof_i, f32[64,512]{1,0:T(8,128)} %get-tuple-element.52.gram_o, ...), custom_call_target="tpu_custom_call" | custom-call | flops 10000000000 | bytes 1048576 | tf_op jit(solution)/shard_map/weight_sums/pallas_call | solution.py:641
  274.4 1.6 round.1
  276.0 1.2 reduce

commit v4 on v3

--- a/solution.py
+++ b/solution.py
@@ -125,14 +125,14 @@
     return pl.BlockSpec(shape, index_map)
 
 
-def front_kernel(n_dap, z_own, dy_ref, m_own, w_in, w_out, w_gate, v_is, v_io, v_os, v_oo, v_bo, v_bg, v_bi,
+def front_kernel(n_dap, z_own, dy_ref, m_own, mask_in, w_in, w_out, w_gate, v_is, v_io, v_os, v_oo, v_bo, v_bg, v_bi,
                  da_ref, keep_ref, got_ref, dgl_ref, gram_ref, dbg_ref, dbo_ref, dsc_ref, dof_ref, wg_ref, sc_ref, off_ref,
-                 sv_ref, give_ref, z_far, m_far, a_all, b_pair, a_sib, lg_ref, dyt_ref, do_out, do_in,
+                 sv_ref, give_ref, z_far, m_far, a_all, b_pair, a_sib, lg_ref, dyt_ref, do_out, do_in, relay, mask16,
                  wk_ref, bias_ref, perm_ref, wo_ref, wot_ref, bout_ref, osc_ref, ooff_ref,
-                 o_s, gram_s, lg_v, dyt_v, do_v, dgl_v, send_sem, recv_sem, loc_sem):
+                 o_s, gram_s, lg_v, dyt_v, do_v, dgl_v, mask_v, send_sem, recv_sem, loc_sem):
     n_chip = n_dap // TWO
     _, rows, cz, cols = z_own.shape
-    z_ref, mask_ref = z_own.at[ZERO], m_own.at[ZERO]
+    z_ref = z_own.at[ZERO]
     chans = a_all.shape[ONE]
     half = chans // TWO
     hr = rows // TWO
@@ -158,7 +158,7 @@
     pl.semaphore_wait(barrier, n_dap - ONE)
 
     n_grp = rows // grp
-    masks = [copy(i, mask_ref, m_far.at[i], hop, ZERO) for i, hop in enumerate((ONE, -ONE, TWO))]
+    masks = [copy(i, mask16, m_far.at[i], hop, ZERO) for i, hop in enumerate((ONE, -ONE, TWO))]
     quarter = lambda q: pl.ds(pl.multiple_of(q * grp, grp), grp)
     z_r = lambda q: copy(3 + q, z_ref.at[quarter(q)], z_far.at[ZERO, quarter(q)], ONE, ZERO)
     z_l = lambda q: copy(3 + n_grp + q, z_ref.at[quarter(q)], z_far.at[ONE, quarter(q)], -ONE, ZERO)
@@ -177,13 +177,19 @@
     back = (OWN, RIGHT, LEFT, OPP)
     ship = [[None if (r == OWN and side == ZERO) else
              copy(base_s + TWO * r + side, do_out.at[r, pl.ds(side * half, half)], do_in.at[back[r], side], HOPS[r], side) for side in (ZERO, ONE)] for r in range(4)]
+    onward = []
     swap_d = [copy(base_s + 8 + q, give_ref.at[pl.ds(q * (half // TWO), half // TWO)], got_ref.at[pl.ds(q * (half // TWO), half // TWO)], ZERO, ONE) for q in (ZERO, ONE)]
 
-    for c in masks:
-        c.start()
     for q in range(n_grp):
         z_r(q).start()
         z_l(n_grp - ONE - q).start()
+        if q == ZERO:
+            mask_v[...] = mask_in[...].astype(BF16)
+            put = pltpu.make_async_copy(mask_v, mask16, loc_sem.at[ZERO])
+            put.start()
+            put.wait()
+            for c in masks:
+                c.start()
     b_all = v_bi[...]
     vecs = [ref[...] for ref in (v_is, v_io, v_os, v_oo, v_bo, v_bg)] + [b_all[:, i * chans:(i + ONE) * chans] for i in range(4)]
     build_weights(core, w_in, w_out, w_gate, vecs, wk_ref, wg_ref, bias_ref, sc_ref, off_ref, perm_ref, wo_ref, wot_ref, bout_ref, osc_ref, ooff_ref)
@@ -196,7 +202,7 @@
         a_parts, b_parts = [], []
         for h in range(TWO):
             rws = slice(h * SUB, (h + ONE) * SUB)
-            act_a, act_b, _ = project(z_b[ZERO, rws], m_b[ZERO, rws].astype(F32) * 0.5, wk_ref, bias_ref, sc_ref, off_ref, chans)
+            act_a, act_b, _ = project(z_b[ZERO, rws], m_b[ZERO].astype(F32)[rws] * 0.5, wk_ref, bias_ref, sc_ref, off_ref, chans)
             a_parts.append(act_a)
             b_parts.append(act_b)
         a_b[ZERO] = jnp.concatenate(a_parts, axis=ONE).astype(BF16)
@@ -254,8 +260,10 @@
 
     def o_body(a_b, b_b):
         base = pl.program_id(ZERO) * per
-        for c in range(per):
-            o_s[base + c] = nt_dot(a_b[c], b_b[c])
+        for c in range(ZERO, per, TWO):
+            both = nt_dot(a_b[c:c + TWO].reshape(TWO * rows, cols), b_b[c:c + TWO].reshape(TWO * jb, cols))
+            o_s[base + c] = both[:rows, :jb]
+            o_s[base + c + ONE] = both[rows:, jb:]
 
     def chain(r):
         where = lax.rem(chip + (HOPS[r] + n_chip), n_chip)
@@ -364,11 +372,11 @@
     diag = lax.broadcasted_iota(jnp.int32, (n, n), ZERO) % SUB == lax.broadcasted_iota(jnp.int32, (n, n), ONE) % SUB
     gram_ref[...] = jnp.sum(jnp.where(diag, gram, 0.0).reshape(chans, SUB, n), axis=ONE)
 
-    pc = 4
+    pc = 8
     n_a = chans // pc
 
     def da_body(do_b, b_b, da_b):
-        for c in range(pc):
+        for c in range(da_b.shape[ZERO]):
             lhs = jnp.concatenate([do_b[r, c] for r in range(4)], axis=ONE)
             rhs = jnp.concatenate([b_b[r, c] for r in range(4)], axis=ZERO)
             da_b[c] = nn_dot(lhs, rhs).astype(BF16)
@@ -378,6 +386,7 @@
         in_specs=[blk((4, pc, rows, jb), lambda s: (ZERO, s, ZERO, ZERO)), blk((4, pc, jb, cols), lambda s: (ZERO, s, ZERO, ZERO))],
         out_specs=[blk((pc, rows, cols), lambda s: (s, ZERO, ZERO))])(do_out, b_pair, da_ref)
 
+    pc = 8
     for r in range(4):
         lax.fori_loop(ZERO, n_grp, lambda q, carry, r=r: (swap_a(r, q).wait_recv(), carry)[ONE], ZERO)
         for c in ship[r]:
@@ -407,7 +416,7 @@
         swap_d[q].start()
     for c in swap_d:
         c.wait_recv()
-    for c in masks + swap_d + [c for pair in ship for c in pair if c is not None]:
+    for c in masks + swap_d + onward + [c for pair in ship for c in pair if c is not None]:
         c.wait_send()
 
     def sent(q, carry):
@@ -606,7 +615,7 @@
     f32 = lambda *shape: sds(shape, F32)
     any_spec = pl.BlockSpec(memory_space=pl.ANY)
     vmem = pl.BlockSpec(memory_space=pltpu.VMEM)
-    n_copy = 3 + 3 * n_grp + 8 * n_grp + 4 * n_grp + 10
+    n_copy = 15 + 15 * n_grp
     acc = f32(ch, SUB, LANES)
     blocks = pltpu.VMEM((ch * SUB, cz * SUB), BF16)
     spread = pltpu.VMEM((ch, SUB, LANES), F32)
@@ -614,17 +623,18 @@
         functools.partial(front_kernel, n_dap), name='front',
         out_shape=(b16(ch, rows, cols), b16(half, rows, cols), b16(half, rows, cols), b16(cz, rows, cols), f32(ch, cz * SUB), acc, acc, acc, acc,
                    b16(SUB * cz, n_e * SUB), f32(cz, cols), f32(cz, cols),
-                   f32(4, ch, rows, cols), b16(half, rows, cols), b16(3, rows, cz, cols), sds((3, rows, cols), jnp.int32), b16(4, ch, rows, cols), b16(4, ch, jb, cols),
-                   b16(4, half, rows, cols), f32(cz, rows, cols), b16(cz, rows, cols), b16(4, ch, rows, jb), b16(4, TWO, half, rows, jb)),
-        in_specs=[any_spec] * 3 + [vmem] * 10,
-        out_specs=(any_spec,) * 4 + (vmem,) * 8 + (any_spec,) * 11,
+                   f32(4, ch, rows, cols), b16(half, rows, cols), b16(3, rows, cz, cols), b16(3, rows, cols), b16(4, ch, rows, cols), b16(4, ch, jb, cols),
+                   b16(4, half, rows, cols), f32(cz, rows, cols), b16(cz, rows, cols), b16(4, ch, rows, jb), b16(4, TWO, half, rows, jb), b16(TWO, half, rows, jb), b16(rows, cols)),
+        in_specs=[any_spec] * 3 + [vmem] * 11,
+        out_specs=(any_spec,) * 4 + (vmem,) * 8 + (any_spec,) * 13,
         scratch_shapes=[pltpu.VMEM((n_e * SUB, SUB * cz), BF16), pltpu.VMEM((n_e, SUB, LANES), F32), blocks, blocks, blocks, spread, spread, spread,
                         pltpu.VMEM((ch, rows, jb), F32), pltpu.VMEM((ch * SUB, cz * SUB), F32), pltpu.VMEM((cz, rows, jb), F32),
                         pltpu.VMEM((cz, rows, jb), BF16), pltpu.VMEM((ch, rows, jb), BF16), pltpu.VMEM((cz, rows, jb), BF16),
+                        pltpu.VMEM((rows, cols), BF16),
                         pltpu.SemaphoreType.DMA((n_copy,)), pltpu.SemaphoreType.DMA((n_copy,)), pltpu.SemaphoreType.DMA((TWO,))],
         cost_estimate=pl.CostEstimate(flops=10**11, bytes_accessed=TWO**20, transcendentals=ZERO),
         compiler_params=pltpu.CompilerParams(vmem_limit_bytes=VMEM_LIMIT, collective_id=ZERO, has_side_effects=True),
-    )(z_t[None], dy_t, mask_loc[None], w_in, w_out, w_gate, *vecs)
+    )(z_t[None], dy_t, mask_loc[None], mask_loc, w_in, w_out, w_gate, *vecs)
     da, keep, got, dgl, gram_o, dbg, dbo, dsc_o, dof_o, wg, sc_in, off_in, sv = outs[:13]
 
     args = (z_t, dy_t, mask_loc, da, keep, got, dgl, sv, wg, sc_in, off_in)

time: 279 us -> 275 us (0.986)
  Pallas kernels: 274 us -> 271 us
    pallas_call x1, Pallas kernels: 222 us -> 219 us  [local_grads(): pl.pallas_call(functools.partial(front_kernel, n_dap), name='front', out_...]
where the time goes in v4:
time: 275 us; the launch traced here: 274 us
  Pallas kernels  271 us (99%)
    pallas_call x1, Pallas kernels, local_grads(): pl.pallas_call(functools.partial(front_kernel, n_dap), name='front', out_...  219 us
    pallas_call x2, Pallas kernels, call(): pl.pallas_call(kernel, name=name, cost_estimate=cost, compiler_params=plt...  38.4 us
    pallas_call x1, Pallas kernels, local_grads(): pl.pallas_call(functools.partial(sum_kernel, n_dap), name='weight_sums',...  13.6 us

profile of v4, /device:TPU:112, one launch (start us, length us, event | category | flops | bytes accessed | tf_op | source)
XLA Modules:
  0.0 273.6 jit_solution(9876715018311405747)
XLA Ops:
  0.6 1.2 reshape.70.v_bi
  1.9 218.5 %front.1 = (bf16[64,64,512]{2,1,0:T(8,128)(2,1)}, bf16[32,64,512]{2,1,0:T(8,128)(2,1)}, bf16[32,64,512]{2,1,0:T(8,128)(2,1)}, bf16[64,64,512]{2,1,0:T(8,128)(2,1...) custom-call(bf16[1,64,64,512]{3,2,1,0:T(8,128)(2,1)} %bitcast.18, ...), custom_call_target="tpu_custom_call" | custom-call | flops 99999997952 | bytes 1048576 | tf_op jit(solution)/shard_map/front/pallas_call | solution.py:622
  220.4 36.8 %input_side.1 = (bf16[64,64,512]{2,1,0:T(8,128)(2,1)}, f32[64,2560]{1,0:T(8,128)}, f32[256,8,128]{2,1,0:T(8,128)}, f32[64,512]{1,0:T(8,128)}, f32[64,512]{1,0:T(8,128)}) custom-call(bf16[64,64,512]{2,1,0:T(8,128)(2,1)} %bitcast.19, bf16[64,64,512]{2,1,0:T(8,128)(2,1)} %bitcast.21, s32[64,512]{1,0:T(8,128)} %mask_ref.1, ...), custom_call_target="tpu_custom_call" | custom-call | flops 20999999488 | bytes 1048576 | tf_op jit(solution)/shard_map/input_side/pallas_call | solution.py:595
  257.2 13.6 %weight_sums.1.tot_ref = f32[256,128]{1,0:T(8,128)} custom-call(f32[64,2560]{1,0:T(8,128)} %get-tuple-element.48.gram_i, f32[256,8,128]{2,1,0:T(8,128)} %get-tuple-element.49.dbias, f32[64,512]{1,0:T(8,128)} %get-tuple-element.50.dsc_i, f32[64,512]{1,0:T(8,128)} %get-tuple-element.51.dof_i, f32[64,512]{1,0:T(8,128)} %get-tuple-element.52.gram_o, ...), custom_call_target="tpu_custom_call" | custom-call | flops 10000000000 | bytes 1048576 | tf_op jit(solution)/shard_map/weight_sums/pallas_call | solution.py:651
  270.8 1.6 round.1
  272.4 1.2 reduce
